TPU v7x, 512 devices: a whole 4x8x8 slice. The times are simulated.
512 devices in a mesh: atoms: 64 (over x, y, core), chan: 8 (over z).
Axes of the slice: x: 4, y: 8, z: 8, core: 2. Of those that a mesh axis runs over, the one named last changes fastest.
Arguments:
- features: bfloat16 [128, 32768], P('chan', 'atoms'), may hold values from -6 to 6
- positions: float32 [3, 32768], P(None, 'atoms'), may hold values from 0 to 384
- block_counts: int32 [256], P('atoms'), may hold values from 64 to 128
- radial_w: float32 [8, 3, 128], P(None, None, 'chan'), may hold values from -2 to 2
- mix_w: bfloat16 [4, 128, 128], replicated, may hold values from -0.25 to 0.25
- read_w: float32 [128], P('chan'), may hold values from -0.5 to 0.5
- ghost_lists: int32 [64, 2, 2], P('atoms'), may hold values from 0 to 3, as said below
- tile_pairs: int32 [64, 24, 2], P('atoms'), may hold values from 0 to 7, as said below
- tile_count: int32 [64], P('atoms'), may hold values from 9 to 24, as said below
Outputs:
- updated: bfloat16 [128, 32768], P('chan', 'atoms')
- energies: float32 [32768], P('atoms')
- scale: float32 [], replicated
Inputs may be any that keep to these rules, and one draw needn't show every extreme that they name: `ghost_lists`: row 0 of group g lists each of its even-numbered blocks once and row 1 each odd-numbered block once, in some order. `tile_pairs`: codes below 4 name the group's own block, codes 4 to 5 a slot of the previous group's ghost_lists row 1, higher codes a slot of the next group's row 0; no code points outside the first or last group. Tile t < 4 of each group is (t, t). Tiles from tile_count[g] on are (0, 0). `tile_count`: some group has 24 live tiles.
All inputs are finite; a program needn't handle non-finite values.
Results may differ from a plain program's by a relative error of at most 0.007.
Values may be sent and summed in bfloat16 or wider, within the bound.
A program may use at most 64 MiB of HBM per device.

v0:
```python
import jax
import jax.numpy as jnp
from jax import lax
from jax.sharding import PartitionSpec as P

NR = 8


root_three = 3.0**0.5
root_fifteen = 15.0**0.5
half_root_five = 0.5 * 5.0**0.5
half_root_fifteen = 0.5 * 15.0**0.5
cutoff_square = 9.0
soften = 0.25
center_step = 3.0 / 7.0
radial_sharp = 2.0
tiles_per_turn = 4


def extended(block, sides, width):
    for axis, dim in sides:
        count = lax.axis_size(axis)
        forward = [(i, i + 1) for i in range(count - 1)]
        backward = [(target, source) for source, target in forward]
        low = lax.ppermute(
            lax.slice_in_dim(block, block.shape[dim] - width, None, axis=dim), axis, forward
        )
        high = lax.ppermute(lax.slice_in_dim(block, 0, width, axis=dim), axis, backward)
        block = jnp.concatenate([low, block, high], axis=dim)
    return block


def split_up(x, dim, count):
    lengths = x.shape
    tiles = x.reshape(*lengths[:dim], count, lengths[dim] // count, *lengths[dim + 1 :])
    return jnp.moveaxis(tiles, dim, 0)


def sent_and_summed(x, axis, dim):
    count = lax.axis_size(axis)
    tiles = lax.all_to_all(split_up(x, dim, count), axis, 0, 0, tiled=True)
    return jnp.sum(tiles.astype(jnp.float32), axis=0)


def copy_for_each(x, axis):
    copies = jnp.broadcast_to(x, (lax.axis_size(axis), *x.shape))
    return lax.all_to_all(copies, axis, split_axis=0, concat_axis=0, tiled=True)


def of_everyone(x, axis):
    return copy_for_each(x, axis).sum(axis=0)


def packed_total(arrays, axis):
    ends = [0]
    for a in arrays:
        ends.append(ends[-1] + a.size)
    running = of_everyone(jnp.concatenate([a.ravel() for a in arrays]), axis)
    return tuple((running[b:e].reshape(a.shape) for a, b, e in zip(arrays, ends, ends[1:])))


def harmonics(unit_x, unit_y, unit_z):
    return jnp.stack(
        [
            jnp.ones_like(unit_x),
            root_three * unit_x,
            root_three * unit_y,
            root_three * unit_z,
            root_fifteen * unit_x * unit_y,
            root_fifteen * unit_y * unit_z,
            half_root_five * (2.0 * unit_z * unit_z - unit_x * unit_x - unit_y * unit_y),
            root_fifteen * unit_x * unit_z,
            half_root_fifteen * (unit_x * unit_x - unit_y * unit_y),
        ]
    )


def tile_kernel(pos_recv, pos_send, self_pair):
    offset = pos_send[:, None, :] - pos_recv[:, :, None]
    dist_sq = jnp.sum(offset * offset, axis=0)
    block_width = dist_sq.shape[0]
    diagonal = (
        lax.broadcasted_iota(jnp.int32, (block_width, block_width), 0)
        == lax.broadcasted_iota(jnp.int32, (block_width, block_width), 1)
    ).astype(jnp.float32)
    cutoff = jnp.square(jnp.maximum(1.0 - dist_sq / cutoff_square, 0.0)) * (
        1.0 - self_pair * diagonal
    )
    distance = jnp.sqrt(dist_sq + soften)
    unit = offset / distance
    angular = harmonics(unit[0], unit[1], unit[2]) * cutoff
    centers = jnp.arange(NR, dtype=jnp.float32) * center_step
    radial = jnp.exp(-radial_sharp * jnp.square(distance[None] - centers[:, None, None]))
    return (radial[:, None] * angular[None]).astype(jnp.bfloat16)


def tile_term(pos_recv, pos_send, sender_rows, self_pair, table):
    kernel = tile_kernel(pos_recv, pos_send, self_pair)
    partial_sums = jnp.einsum(
        "cj,kmij->ckmi", sender_rows, kernel, preferred_element_type=jnp.float32
    )
    return jnp.einsum("kmc,ckmi->cmi", table, partial_sums, precision=lax.Precision.HIGHEST)


def invariants(density):
    first = density[:, 0]
    return jnp.stack(
        [
            first,
            first * first,
            jnp.sum(jnp.square(density[:, 1:4]), axis=1),
            jnp.sum(jnp.square(density[:, 4:9]), axis=1),
        ]
    )


def per_device(
    features, positions, block_counts, radial_w, mix_w, read_w, ghost_lists, tile_pairs, tile_count
):
    local_chan = features.shape[0]
    blocks = block_counts.shape[0]
    local_atoms = positions.shape[1]
    block_width = local_atoms // blocks
    ghosts = ghost_lists.shape[2]
    present = (jnp.arange(block_width, dtype=jnp.int32)[None, :] < block_counts[:, None]).astype(
        jnp.float32
    )
    present_flat = present.reshape(-1)
    senders = (features.astype(jnp.float32) * present_flat[None, :]).astype(jnp.bfloat16)
    own_where = positions.reshape(3, blocks, block_width)
    send_lists = ghost_lists[0]
    list_row = jnp.concatenate(
        [
            send_lists.reshape(-1).astype(jnp.float32),
            jnp.zeros((local_atoms - 2 * ghosts,), jnp.float32),
        ]
    )
    place_rows = jnp.concatenate([positions, list_row[None, :]], axis=0)
    widened = extended(senders, (("atoms", 1),), local_atoms)
    wide_places = extended(place_rows, (("atoms", 1),), local_atoms)
    source_rows = widened.reshape(local_chan, 3 * blocks, block_width)
    source_where = wide_places[:3].reshape(3, 3 * blocks, block_width)
    left_list = wide_places[3, ghosts : 2 * ghosts].astype(jnp.int32)
    right_list = wide_places[3, 2 * local_atoms : 2 * local_atoms + ghosts].astype(jnp.int32)
    lookup = jnp.concatenate(
        [blocks + jnp.arange(blocks, dtype=jnp.int32), left_list, 2 * blocks + right_list]
    )
    degree = jnp.array([0, 1, 1, 1, 2, 2, 2, 2, 2], dtype=jnp.int32)
    table = jnp.take(radial_w, degree, axis=1)
    tile_list = tile_pairs[0]
    tile_total = tile_count[0]
    batched = jax.vmap(tile_term, in_axes=(1, 1, 1, 0, None))

    def one_turn(turn, totals):
        tile_ids = turn * tiles_per_turn + jnp.arange(tiles_per_turn, dtype=jnp.int32)
        receivers = tile_list[tile_ids, 0]
        codes = tile_list[tile_ids, 1]
        weights = (tile_ids < tile_total).astype(jnp.float32)
        picked = jnp.take(source_rows, lookup[codes], axis=1)
        picked_where = jnp.take(source_where, lookup[codes], axis=1)
        pos_recv = jnp.take(own_where, receivers, axis=1)
        self_pairs = ((codes < blocks) & (codes == receivers)).astype(jnp.float32)
        terms = batched(pos_recv, picked_where, picked, self_pairs, table)
        return totals.at[receivers].add(terms * weights[:, None, None, None])

    start = jnp.zeros((blocks, local_chan, 9, block_width), jnp.float32)
    totals = lax.fori_loop(0, tile_list.shape[0] // tiles_per_turn, one_turn, start)
    density = totals.transpose(1, 2, 0, 3).reshape(local_chan, 9, local_atoms)
    basis = invariants(density).astype(jnp.bfloat16)
    chan_start = lax.axis_index("chan") * local_chan
    my_inputs = lax.dynamic_slice_in_dim(mix_w, chan_start, local_chan, 1)
    weights = my_inputs
    mixed = sent_and_summed(
        jnp.einsum("qco,qca->oa", weights, basis, preferred_element_type=jnp.float32).astype(
            jnp.bfloat16
        ),
        "chan",
        0,
    )
    hidden = features.astype(jnp.float32) + jax.nn.silu(mixed)
    updated = (hidden * present_flat[None, :]).astype(jnp.bfloat16)
    local_energy = jnp.dot(read_w, hidden, precision=lax.Precision.HIGHEST)
    energy = of_everyone(local_energy, "chan")
    total_square, total_atoms = packed_total(
        (jnp.sum(present_flat * energy * energy), jnp.sum(present_flat)), "atoms"
    )
    scale = jnp.sqrt(1.0 + total_square / total_atoms)
    return (updated, energy * present_flat / scale, scale)


def solution(mesh):
    in_specs = (
        P("chan", "atoms"),
        P(None, "atoms"),
        P("atoms"),
        P(None, None, "chan"),
        P(),
        P("chan"),
        P("atoms", None, None),
        P("atoms", None, None),
        P("atoms"),
    )
    out_specs = (P("chan", "atoms"), P("atoms"), P())
    return jax.shard_map(
        per_device, mesh=mesh, in_specs=in_specs, out_specs=out_specs, check_vma=False
    )
```

profile of v0, /device:TPU:1, one launch (start us, length us, event | category | flops | bytes accessed | tf_op | source)
XLA Modules:
  0.0 203.9 jit_solution(9674050361763198324)
XLA Ops:
  2.1 4.6 %collective-permute-start.2 = (bf16[16,512]{1,0:T(8,128)(2,1)S(1)}, bf16[16,512]{1,0:T(8,128)(2,1)S(1)}, u32[]{:S(2)}, u32[]{:S(2)}) collective-permute-start(bf16[16,512]{1,0:T(8,128)(2,1)S(1)} %fusion.33), channel_id=1, source_target_pairs={{0,8},{8,16},{16,24},{24,32},{32,40},{40,48},{48,56},{56,64},{64,7... | collective-permute-start | bytes 49160 | tf_op jit(solution)/shard_map/ppermute | solution.py:25
  6.7 5.5 %collective-permute-start.3 = (bf16[16,512]{1,0:T(8,128)(2,1)S(1)}, bf16[16,512]{1,0:T(8,128)(2,1)S(1)}, u32[]{:S(2)}, u32[]{:S(2)}) collective-permute-start(bf16[16,512]{1,0:T(8,128)(2,1)S(1)} %fusion.33), channel_id=1, source_target_pairs={{8,0},{16,8},{24,16},{32,24},{40,32},{48,40},{56,48},{64,56},{72,6... | collective-permute-start | bytes 49160 | tf_op jit(solution)/shard_map/ppermute | solution.py:28
  13.7 1.9 collective-permute-start
  15.6 2.4 %collective-permute-start.1 = (f32[4,512]{1,0:T(4,128)S(1)}, f32[4,512]{1,0:T(4,128)S(1)}, u32[]{:S(2)}, u32[]{:S(2)}) collective-permute-start(f32[4,512]{1,0:T(4,128)S(1)} %pad_maximum_fusion.3), channel_id=1, source_target_pairs={{8,0},{16,8},{24,16},{32,24},{40,32},{48,40},{56,48},{64,56},{72,6... | collective-permute-start | bytes 24584 | tf_op jit(solution)/shard_map/ppermute | solution.py:28
  21.5 124.9 %while.13 = (s32[]{:T(128)}, f32[4,16,9,128]{3,1,2,0:T(8,128)S(1)}, s32[24,2]{0,1:T(2,128)}, s32[8]{0:T(128)S(1)}, bf16[16,12,128]{2,0,1:T(8,128)(2,1)S(1)}, /*i...) while((s32[]{:T(128)}, f32[4,16,9,128]{3,1,2,0:T(8,128)S(1)}, ...), condition=%wide.region_3.4_spmd, body=%wide.region_0.3_spmd.sunk | while | flops 172619936 | bytes 26691816 | solution.py:167
  28.2 1.7 multiply_exponential_fusion.2
  30.5 5.6 %fusion.73 = f32[4,16,8,9,128]{4,1,3,2,0:T(8,128)} fusion(f32[4,9,128,128]{3,2,1,0:T(8,128)S(1)} %broadcast_multiply_fusion.2, f32[4,8,128,128]{3,2,1,0:T(8,128)} %multiply_exponential_fusion.2, bf16[4,16,128]{2,1,0:T(8,128)(2,1)S(1)} %gather_fusion.5, pred[4]{0:T(512)(128)(4,1)S(1)} %compare_and_fusion.3), kind=kOutput, calls=%fused_computation.9.clone.1 | convolution fusion | flops 160440320 | bytes 6832132 | tf_op jit(solution)/shard_map/while/body/eval_jaxpr/vmap(cj,kmij->ckmi)/dot_general | solution.py:99
  36.2 4.5 %fusion.74 = f32[16,9,1,4,128]{4,2,3,1,0:T(1,128)S(1)} fusion(f32[8,9,16,1,1]{0,3,4,1,2:T(1,128)S(1)} %copy.44, f32[4,16,8,9,128]{4,1,3,2,0:T(8,128)} %fusion.73), kind=kOutput, calls=%fused_computation.12.clone.1 | convolution fusion | flops 7077888 | bytes 2658816 | tf_op jit(solution)/shard_map/while/body/eval_jaxpr/vmap(kmc,ckmi->cmi)/dot_general | solution.py:102
  42.4 1.3 gather_fusion
  49.0 1.7 multiply_exponential_fusion.2
  51.3 5.6 %fusion.73 = f32[4,16,8,9,128]{4,1,3,2,0:T(8,128)} fusion(f32[4,9,128,128]{3,2,1,0:T(8,128)S(1)} %broadcast_multiply_fusion.2, f32[4,8,128,128]{3,2,1,0:T(8,128)} %multiply_exponential_fusion.2, bf16[4,16,128]{2,1,0:T(8,128)(2,1)S(1)} %gather_fusion.5, pred[4]{0:T(512)(128)(4,1)S(1)} %compare_and_fusion.3), kind=kOutput, calls=%fused_computation.9.clone.1 | convolution fusion | flops 160440320 | bytes 6832132 | tf_op jit(solution)/shard_map/while/body/eval_jaxpr/vmap(cj,kmij->ckmi)/dot_general | solution.py:99
  57.0 4.5 %fusion.74 = f32[16,9,1,4,128]{4,2,3,1,0:T(1,128)S(1)} fusion(f32[8,9,16,1,1]{0,3,4,1,2:T(1,128)S(1)} %copy.44, f32[4,16,8,9,128]{4,1,3,2,0:T(8,128)} %fusion.73), kind=kOutput, calls=%fused_computation.12.clone.1 | convolution fusion | flops 7077888 | bytes 2658816 | tf_op jit(solution)/shard_map/while/body/eval_jaxpr/vmap(kmc,ckmi->cmi)/dot_general | solution.py:102
  63.2 1.3 gather_fusion
  69.9 1.7 multiply_exponential_fusion.2
  72.2 5.6 %fusion.73 = f32[4,16,8,9,128]{4,1,3,2,0:T(8,128)} fusion(f32[4,9,128,128]{3,2,1,0:T(8,128)S(1)} %broadcast_multiply_fusion.2, f32[4,8,128,128]{3,2,1,0:T(8,128)} %multiply_exponential_fusion.2, bf16[4,16,128]{2,1,0:T(8,128)(2,1)S(1)} %gather_fusion.5, pred[4]{0:T(512)(128)(4,1)S(1)} %compare_and_fusion.3), kind=kOutput, calls=%fused_computation.9.clone.1 | convolution fusion | flops 160440320 | bytes 6832132 | tf_op jit(solution)/shard_map/while/body/eval_jaxpr/vmap(cj,kmij->ckmi)/dot_general | solution.py:99
  77.9 4.5 %fusion.74 = f32[16,9,1,4,128]{4,2,3,1,0:T(1,128)S(1)} fusion(f32[8,9,16,1,1]{0,3,4,1,2:T(1,128)S(1)} %copy.44, f32[4,16,8,9,128]{4,1,3,2,0:T(8,128)} %fusion.73), kind=kOutput, calls=%fused_computation.12.clone.1 | convolution fusion | flops 7077888 | bytes 2658816 | tf_op jit(solution)/shard_map/while/body/eval_jaxpr/vmap(kmc,ckmi->cmi)/dot_general | solution.py:102
  84.0 1.3 gather_fusion
  90.7 1.7 multiply_exponential_fusion.2
  93.0 5.6 %fusion.73 = f32[4,16,8,9,128]{4,1,3,2,0:T(8,128)} fusion(f32[4,9,128,128]{3,2,1,0:T(8,128)S(1)} %broadcast_multiply_fusion.2, f32[4,8,128,128]{3,2,1,0:T(8,128)} %multiply_exponential_fusion.2, bf16[4,16,128]{2,1,0:T(8,128)(2,1)S(1)} %gather_fusion.5, pred[4]{0:T(512)(128)(4,1)S(1)} %compare_and_fusion.3), kind=kOutput, calls=%fused_computation.9.clone.1 | convolution fusion | flops 160440320 | bytes 6832132 | tf_op jit(solution)/shard_map/while/body/eval_jaxpr/vmap(cj,kmij->ckmi)/dot_general | solution.py:99
  98.7 4.5 %fusion.74 = f32[16,9,1,4,128]{4,2,3,1,0:T(1,128)S(1)} fusion(f32[8,9,16,1,1]{0,3,4,1,2:T(1,128)S(1)} %copy.44, f32[4,16,8,9,128]{4,1,3,2,0:T(8,128)} %fusion.73), kind=kOutput, calls=%fused_computation.12.clone.1 | convolution fusion | flops 7077888 | bytes 2658816 | tf_op jit(solution)/shard_map/while/body/eval_jaxpr/vmap(kmc,ckmi->cmi)/dot_general | solution.py:102
  111.5 1.7 multiply_exponential_fusion.2
  113.8 5.6 %fusion.73 = f32[4,16,8,9,128]{4,1,3,2,0:T(8,128)} fusion(f32[4,9,128,128]{3,2,1,0:T(8,128)S(1)} %broadcast_multiply_fusion.2, f32[4,8,128,128]{3,2,1,0:T(8,128)} %multiply_exponential_fusion.2, bf16[4,16,128]{2,1,0:T(8,128)(2,1)S(1)} %gather_fusion.5, pred[4]{0:T(512)(128)(4,1)S(1)} %compare_and_fusion.3), kind=kOutput, calls=%fused_computation.9.clone.1 | convolution fusion | flops 160440320 | bytes 6832132 | tf_op jit(solution)/shard_map/while/body/eval_jaxpr/vmap(cj,kmij->ckmi)/dot_general | solution.py:99
  119.5 4.5 %fusion.74 = f32[16,9,1,4,128]{4,2,3,1,0:T(1,128)S(1)} fusion(f32[8,9,16,1,1]{0,3,4,1,2:T(1,128)S(1)} %copy.44, f32[4,16,8,9,128]{4,1,3,2,0:T(8,128)} %fusion.73), kind=kOutput, calls=%fused_computation.12.clone.1 | convolution fusion | flops 7077888 | bytes 2658816 | tf_op jit(solution)/shard_map/while/body/eval_jaxpr/vmap(kmc,ckmi->cmi)/dot_general | solution.py:102
  132.3 1.7 multiply_exponential_fusion.2
  134.6 5.6 %fusion.73 = f32[4,16,8,9,128]{4,1,3,2,0:T(8,128)} fusion(f32[4,9,128,128]{3,2,1,0:T(8,128)S(1)} %broadcast_multiply_fusion.2, f32[4,8,128,128]{3,2,1,0:T(8,128)} %multiply_exponential_fusion.2, bf16[4,16,128]{2,1,0:T(8,128)(2,1)S(1)} %gather_fusion.5, pred[4]{0:T(512)(128)(4,1)S(1)} %compare_and_fusion.3), kind=kOutput, calls=%fused_computation.9.clone.1 | convolution fusion | flops 160440320 | bytes 6832132 | tf_op jit(solution)/shard_map/while/body/eval_jaxpr/vmap(cj,kmij->ckmi)/dot_general | solution.py:99
  140.3 4.5 %fusion.74 = f32[16,9,1,4,128]{4,2,3,1,0:T(1,128)S(1)} fusion(f32[8,9,16,1,1]{0,3,4,1,2:T(1,128)S(1)} %copy.44, f32[4,16,8,9,128]{4,1,3,2,0:T(8,128)} %fusion.73), kind=kOutput, calls=%fused_computation.12.clone.1 | convolution fusion | flops 7077888 | bytes 2658816 | tf_op jit(solution)/shard_map/while/body/eval_jaxpr/vmap(kmc,ckmi->cmi)/dot_general | solution.py:102
  146.8 16.2 %all_to_all.17 = bf16[8,16,512]{2,1,0:T(8,128)(2,1)S(1)} all-to-all(bf16[8,16,512]{2,1,0:T(8,128)(2,1)S(1)} %bitcast.112), channel_id=1, replica_groups=mesh['atoms'=64,'chan'=8] {'chan'}, dimensions={0} | all-to-all | bytes 262144 | tf_op jit(solution)/shard_map/all_to_all | solution.py:41
  163.8 3.3 %all-to-all-start.1 = ((f32[8,1,512]{2,1,0:T(1,128)}), f32[8,1,512]{2,1,0:T(1,128)S(1)}, u32[]{:S(2)}, u32[]{:S(2)}) async-start(f32[8,1,512]{2,1,0:T(1,128)} %broadcast_in_dim.118), calls=%async_computation.1 | async-start | bytes 32768 | tf_op jit(solution)/shard_map/all_to_all | solution.py:47
  167.8 5.9 %all-to-all-done.1 = f32[8,1,512]{2,1,0:T(1,128)S(1)} async-done(((f32[8,1,512]{2,1,0:T(1,128)}), f32[8,1,512]{2,1,0:T(1,128)S(1)}, u32[]{:S(2)}, u32[]{:S(2)}) %all-to-all-start.1) | async-done | bytes 16416 | tf_op jit(solution)/shard_map/all_to_all | solution.py:47
  174.5 1.4 pad_maximum_fusion.4
  176.5 14.3 %all-to-all-start.2 = ((f32[64,1,2]{2,1,0:T(1,128)}), f32[64,1,2]{2,1,0:T(1,128)S(1)}, u32[]{:S(2)}, u32[]{:S(2)}) async-start(f32[64,1,2]{2,1,0:T(1,128)} %broadcast_in_dim.119), calls=%async_computation.2 | async-start | bytes 65536 | tf_op jit(solution)/shard_map/all_to_all | solution.py:47
  191.4 8.7 %all-to-all-done.2 = f32[64,1,2]{2,1,0:T(1,128)S(1)} async-done(((f32[64,1,2]{2,1,0:T(1,128)}), f32[64,1,2]{2,1,0:T(1,128)S(1)}, u32[]{:S(2)}, u32[]{:S(2)}) %all-to-all-start.2) | async-done | bytes 544 | tf_op jit(solution)/shard_map/all_to_all | solution.py:47
  (257 shorter events, 60.0 us)
Async XLA Ops:
  0.6 145.9 %copy-start = (bf16[4,128,128]{2,1,0:T(8,128)(2,1)S(1)}, bf16[4,128,128]{2,1,0:T(8,128)(2,1)}, u32[]{:S(2)}) copy-start(bf16[4,128,128]{2,1,0:T(8,128)(2,1)} %param.16) | copy-start | bytes 393220
  2.1 19.3 %collective-permute-start.2 = (bf16[16,512]{1,0:T(8,128)(2,1)S(1)}, bf16[16,512]{1,0:T(8,128)(2,1)S(1)}, u32[]{:S(2)}, u32[]{:S(2)}) collective-permute-start(bf16[16,512]{1,0:T(8,128)(2,1)S(1)} %fusion.33), channel_id=1, source_target_pairs={{0,8},{8,16},{16,24},{24,32},{32,40},{40,48},{48,56},{56,64},{64,7... | collective-permute-start | bytes 49160 | tf_op jit(solution)/shard_map/ppermute | solution.py:25
  6.7 14.7 %collective-permute-start.3 = (bf16[16,512]{1,0:T(8,128)(2,1)S(1)}, bf16[16,512]{1,0:T(8,128)(2,1)S(1)}, u32[]{:S(2)}, u32[]{:S(2)}) collective-permute-start(bf16[16,512]{1,0:T(8,128)(2,1)S(1)} %fusion.33), channel_id=1, source_target_pairs={{8,0},{16,8},{24,16},{32,24},{40,32},{48,40},{56,48},{64,56},{72,6... | collective-permute-start | bytes 49160 | tf_op jit(solution)/shard_map/ppermute | solution.py:28
  13.7 6.9 %collective-permute-start = (f32[4,512]{1,0:T(4,128)S(1)}, f32[4,512]{1,0:T(4,128)S(1)}, u32[]{:S(2)}, u32[]{:S(2)}) collective-permute-start(f32[4,512]{1,0:T(4,128)S(1)} %pad_maximum_fusion.3), channel_id=1, source_target_pairs={{0,8},{8,16},{16,24},{24,32},{32,40},{40,48},{48,56},{56,64},{64,7... | collective-permute-start | bytes 24584 | tf_op jit(solution)/shard_map/ppermute | solution.py:25
  15.6 5.0 %collective-permute-start.1 = (f32[4,512]{1,0:T(4,128)S(1)}, f32[4,512]{1,0:T(4,128)S(1)}, u32[]{:S(2)}, u32[]{:S(2)}) collective-permute-start(f32[4,512]{1,0:T(4,128)S(1)} %pad_maximum_fusion.3), channel_id=1, source_target_pairs={{8,0},{16,8},{24,16},{32,24},{40,32},{48,40},{56,48},{64,56},{72,6... | collective-permute-start | bytes 24584 | tf_op jit(solution)/shard_map/ppermute | solution.py:28
  21.5 141.5 %copy-start.1 = (bf16[16,512]{1,0:T(8,128)(2,1)S(1)}, bf16[16,512]{1,0:T(8,128)(2,1)}, u32[]{:S(2)}) copy-start(bf16[16,512]{1,0:T(8,128)(2,1)} %param.12) | copy-start | bytes 49156
  21.5 141.5 %copy-start.3 = (f32[16]{0:T(128)S(1)}, f32[16]{0:T(128)}, u32[]{:S(2)}) copy-start(f32[16]{0:T(128)} %param.17) | copy-start | bytes 196
  21.5 145.7 %copy-start.2 = (s32[4]{0:T(128)S(1)}, s32[4]{0:T(128)}, u32[]{:S(2)}) copy-start(s32[4]{0:T(128)} %param.14) | copy-start | bytes 52
  163.8 10.0 %all-to-all-start.1 = ((f32[8,1,512]{2,1,0:T(1,128)}), f32[8,1,512]{2,1,0:T(1,128)S(1)}, u32[]{:S(2)}, u32[]{:S(2)}) async-start(f32[8,1,512]{2,1,0:T(1,128)} %broadcast_in_dim.118), calls=%async_computation.1 | async-start | bytes 32768 | tf_op jit(solution)/shard_map/all_to_all | solution.py:47
  176.5 23.6 %all-to-all-start.2 = ((f32[64,1,2]{2,1,0:T(1,128)}), f32[64,1,2]{2,1,0:T(1,128)S(1)}, u32[]{:S(2)}, u32[]{:S(2)}) async-start(f32[64,1,2]{2,1,0:T(1,128)} %broadcast_in_dim.119), calls=%async_computation.2 | async-start | bytes 65536 | tf_op jit(solution)/shard_map/all_to_all | solution.py:47
where the time goes:
time: 205 us; the launch traced here: 204 us
  matrix products  61.3 us (30%)
  local copies, waits for them, and re-layouts  38 us (19%)
  other arithmetic  36.7 us (18%)
  starting transfers between devices  31.9 us (16%)
  blocking collectives  16.2 us (8%)
  waiting for transfers between devices  15.3 us (7%)
  between operations  3.35 us (2%)
    dot_general x6, matrix products, tile_term(): jnp.einsum('cj,kmij->ckmi', sender_rows, kernel, preferred_element_type=j...  33.8 us
    dot_general x6, matrix products, tile_term(): jnp.einsum('kmc,ckmi->cmi', table, partial_sums, precision=lax.Precision....  27.2 us
    all_to_all x2, starting transfers between devices, copy_for_each(): return lax.all_to_all(copies, axis, split_axis=0, concat_axis=0, tiled=True)  17.6 us
    all_to_all x1, blocking collectives, sent_and_summed(): tiles = lax.all_to_all(split_up(x, dim, count), axis, 0, 0, tiled=True)  16.2 us
    all_to_all x2, waiting for transfers between devices, copy_for_each(): return lax.all_to_all(copies, axis, split_axis=0, concat_axis=0, tiled=True)  14.6 us
    exp x6, other arithmetic, tile_kernel(): jnp.exp(-radial_sharp * jnp.square(distance[None] - centers[:, None, None]))  10.4 us
    gather x6, local copies, waits for them, and re-layouts, one_turn(): receivers = tile_list[tile_ids, 0]  7.96 us
    gather x6, local copies, waits for them, and re-layouts, one_turn(): codes = tile_list[tile_ids, 1]  7.95 us
  transfers between devices with their start and end apart: 6, of which 3 were waited for; matrix products, arithmetic and copies ran while one was open for 3% of the time, Pallas kernels for 0%

commit v1 on v0

v1 whole, which is shorter than its diff:
```python
import functools

import jax
import jax.numpy as jnp
from jax import lax
from jax.experimental import pallas as pl
from jax.experimental.pallas import tpu as pltpu
from jax.sharding import PartitionSpec as P

MESH = pl.DeviceIdType.MESH
NR = 8
NM = 9
BLK = 128
OWN = 4
PAIRS = 14

root_three = 3.0**0.5
root_fifteen = 15.0**0.5
half_root_five = 0.5 * 5.0**0.5
half_root_fifteen = 0.5 * 15.0**0.5
cutoff_square = 9.0
soften = 0.25
center_step = 3.0 / 7.0
radial_sharp = 2.0
degree = (0, 1, 1, 1, 2, 2, 2, 2, 2)
order = (0, 2, 1, 3)
place_of = (0, 2, 1, 3)


def kernel(
    na,
    nc,
    feat_hbm,
    pos_hbm,
    counts_hbm,
    radial_hbm,
    mix_hbm,
    read_hbm,
    ghost_hbm,
    pairs_hbm,
    live_hbm,
    upd_out,
    energy_out,
    scale_out,
    feat,
    halo,
    pos,
    mixv,
    mixt,
    rw,
    rd,
    wst,
    wb,
    readcol,
    meta,
    meta_in,
    spos,
    tmat,
    rpos,
    sendt,
    kt,
    run,
    fown,
    ust_send,
    ust,
    est,
    yst,
    xst,
    counts,
    ghost,
    pairs,
    live_count,
    tile_place,
    slot_tile,
    slot_live,
    keep,
    last_slot,
    local_sem,
    feat_send,
    feat_recv,
    w_send,
    w_recv,
    meta_sem,
    halo_send,
    halo_recv,
    u_send,
    u_recv,
    e_send,
    e_recv,
    y_send,
    y_recv,
    x_send,
    x_recv,
):
    cz = feat_hbm.shape[0]
    tiles = pairs.shape[2]
    rows = BLK // nc
    ny = max(1, min(8, na // 2))
    nx = na // (2 * ny)
    nxc = 2 * nx

    g = lax.axis_index("atoms")
    z = lax.axis_index("chan")
    left, right = lax.rem(g + na - 1, na), lax.rem(g + 1, na)
    xi = g // (2 * ny)
    yi = lax.rem(g // 2, ny)
    ci = lax.rem(g, 2)
    xc = xi * 2 + ci

    def chan_peer(d):
        return (g, lax.rem(z + d, nc))

    def y_peer(d):
        return (xi * (2 * ny) + lax.rem(yi + d, ny) * 2 + ci, z)

    def x_peer(d):
        other = lax.rem(xc + d, nxc)
        return ((other // 2) * (2 * ny) + yi * 2 + lax.rem(other, 2), z)

    own_rows = pl.ds(pl.multiple_of(z * cz, cz), cz)

    local = [
        pltpu.make_async_copy(
            feat_hbm.at[:, pl.ds(BLK * b, BLK)],
            feat.at[own_rows, pl.ds(BLK * n, BLK)],
            local_sem.at[n],
        )
        for n, b in enumerate(order)
    ]
    pos_copy = pltpu.make_async_copy(pos_hbm, pos, local_sem.at[4])
    rw_copy = pltpu.make_async_copy(radial_hbm, rw, local_sem.at[5])
    rd_copy = pltpu.make_async_copy(read_hbm, rd, local_sem.at[6])
    mix_copy = pltpu.make_async_copy(mix_hbm, mixv, local_sem.at[7])
    ints = [
        pltpu.make_async_copy(src, dst, local_sem.at[8 + n])
        for n, (src, dst) in enumerate(
            ((counts_hbm, counts), (ghost_hbm, ghost), (pairs_hbm, pairs), (live_hbm, live_count))
        )
    ]
    pos_copy.start()
    for c in ints:
        c.start()
    for c in local:
        c.start()
    rw_copy.start()
    rd_copy.start()
    mix_copy.start()

    barrier = pltpu.get_barrier_semaphore()
    greeted = 0
    for d in range(1, nc):
        pl.semaphore_signal(barrier, inc=1, device_id=chan_peer(d), device_id_type=MESH)
        greeted += 1
    for other in (left, right):
        pl.semaphore_signal(barrier, inc=1, device_id=(other, z), device_id_type=MESH)
        greeted += 1
    for d in range(1, ny):
        pl.semaphore_signal(barrier, inc=1, device_id=y_peer(d), device_id_type=MESH)
        greeted += 1
    for d in range(1, nxc):
        pl.semaphore_signal(barrier, inc=1, device_id=x_peer(d), device_id_type=MESH)
        greeted += 1

    lane = lax.broadcasted_iota(jnp.int32, (1, BLK), 1)
    for c in ints:
        c.wait()
    pos_copy.wait()
    zero_row = jnp.zeros((1, BLK), jnp.float32)
    boxes = []
    for b in range(OWN):
        where = pos[:, pl.ds(BLK * b, BLK)]
        present = (lane < counts[b]).astype(jnp.float32)
        low = (ghost[0, 0, 0] >> 1).astype(jnp.float32)
        high = (ghost[0, 1, 0] >> 1).astype(jnp.float32)
        rows8 = jnp.concatenate(
            [where, present, zero_row + low, zero_row + high, zero_row, zero_row], axis=0
        )
        boxes.append(rows8)
        spos[b] = rows8
    swap_low = ghost[0, 0, 0] != 0
    swap_high = ghost[0, 1, 0] != 1
    meta[0, 0] = jnp.where(swap_low, boxes[2], boxes[0])
    meta[0, 1] = jnp.where(swap_low, boxes[0], boxes[2])
    meta[1, 0] = jnp.where(swap_high, boxes[3], boxes[1])
    meta[1, 1] = jnp.where(swap_high, boxes[1], boxes[3])

    rw_copy.wait()
    rd_copy.wait()
    folded = jnp.concatenate([rw[:, k, :] for k in range(NR)], axis=1)
    read_row = jnp.concatenate(
        [rd[...].reshape(1, cz), jnp.zeros((1, BLK - cz), jnp.float32)], axis=1
    )
    wst[z] = jnp.concatenate([folded, read_row, jnp.zeros((4, BLK), jnp.float32)], axis=0)

    total = live_count[0]

    def count(t, acc):
        r = pairs[0, 0, t]
        alive = t < total
        rank = jnp.int32(0)
        out = []
        for b in range(OWN):
            hit = jnp.logical_and(alive, r == b)
            rank = jnp.where(hit, acc[b], rank)
            out.append(acc[b] + hit.astype(jnp.int32))
        tile_place[t] = rank
        return tuple(out)

    sizes = lax.fori_loop(0, tiles, count, (jnp.int32(0),) * OWN)
    starts = [jnp.int32(0)]
    for b in range(OWN):
        used = (sizes[b] + 1) >> 1
        last_slot[b] = jnp.maximum(starts[b] + used - 1, 0)
        starts.append(starts[b] + used)

    def settle(t, _):
        r = pairs[0, 0, t]
        first = jnp.int32(0)
        for b in range(OWN):
            first = jnp.where(r == b, starts[b], first)
        spot = 2 * first + tile_place[t]
        tile_place[t] = jnp.where(t < total, spot, -1)
        return 0

    lax.fori_loop(0, tiles, settle, 0)

    def fill(s, _):
        which, alive = jnp.int32(0), jnp.int32(0)
        for t in range(tiles):
            hit = (tile_place[t] == s).astype(jnp.int32)
            which = which + hit * t
            alive = alive + hit
        slot_tile[s] = which
        slot_live[s] = alive
        return 0

    lax.fori_loop(0, 2 * PAIRS, fill, 0)

    def mark(p, _):
        same = jnp.int32(1)
        for b in range(OWN):
            same = jnp.where(starts[b] == p, 0, same)
        keep[p] = same
        return 0

    lax.fori_loop(0, PAIRS, mark, 0)

    tmat[...] = jnp.zeros((BLK, BLK), jnp.float32)
    for b in range(OWN):
        tmat[pl.ds(8 * b, 8), :] = boxes[b]
    tmat[...] = tmat[...].T
    mine = tmat[pl.ds(pl.multiple_of(z * rows, rows), rows), :]
    for b in range(OWN):
        for d in range(3):
            rpos[b, d] = jnp.broadcast_to(mine[:, 8 * b + d : 8 * b + d + 1], (rows, BLK))

    for c in local:
        c.wait()
    pl.semaphore_wait(barrier, greeted)

    def feat_copy(d):
        return pltpu.make_async_remote_copy(
            src_ref=feat.at[own_rows],
            dst_ref=feat.at[own_rows],
            send_sem=feat_send.at[d],
            recv_sem=feat_recv.at[d],
            device_id=chan_peer(d),
            device_id_type=MESH,
        )

    def w_copy(d):
        return pltpu.make_async_remote_copy(
            src_ref=wst.at[z],
            dst_ref=wst.at[z],
            send_sem=w_send.at[d],
            recv_sem=w_recv.at[d],
            device_id=chan_peer(d),
            device_id_type=MESH,
        )

    def meta_copy(side):
        return pltpu.make_async_remote_copy(
            src_ref=meta.at[side],
            dst_ref=meta_in.at[1 - side],
            send_sem=meta_sem.at[side],
            recv_sem=meta_sem.at[3 - side],
            device_id=(left if side == 0 else right, z),
            device_id_type=MESH,
        )

    def halo_copy(side, d):
        part = pl.ds(pl.multiple_of(lax.rem(z + nc - d, nc) * cz, cz), cz)
        return pltpu.make_async_remote_copy(
            src_ref=feat.at[part, pl.ds(2 * BLK * side, 2 * BLK)],
            dst_ref=halo.at[1 - side, part],
            send_sem=halo_send.at[side, d],
            recv_sem=halo_recv.at[1 - side, d],
            device_id=(left if side == 0 else right, z),
            device_id_type=MESH,
        )

    far_first = sorted(range(1, nc), key=lambda d: -min(d, nc - d))
    near_first = far_first[::-1]
    for side in range(2):
        meta_copy(side).start()
    for d in far_first:
        feat_copy(d).start()
    for side in range(2):
        halo_copy(side, 0).start()
    for d in far_first:
        w_copy(d).start()

    for side in range(2):
        meta_copy(side).wait_recv()
    for side in range(2):
        for n in range(2):
            spos[OWN + 2 * side + n] = meta_in[side, n]

    shape = (rows, BLK)
    own_index = lax.broadcasted_iota(jnp.int32, shape, 0) + z * rows
    off_diagonal = (own_index != lax.broadcasted_iota(jnp.int32, shape, 1)).astype(jnp.float32)

    def geometry(p, half):
        s = 2 * p + half
        t = slot_tile[s]
        r = pairs[0, 0, t]
        q = pairs[0, 1, t]
        there = spos[q]
        weight = slot_live[s].astype(jnp.float32)
        own = (q == r).astype(jnp.float32)
        off = [there[d : d + 1, :] - rpos[r, d] for d in range(3)]
        dist_sq = off[0] * off[0] + off[1] * off[1] + off[2] * off[2]
        shut = jnp.square(jnp.maximum(1.0 - dist_sq / cutoff_square, 0.0))
        shut = shut * (1.0 - own * (1.0 - off_diagonal))
        shut = shut * (there[3:4, :] * weight)
        distance = jnp.sqrt(dist_sq + soften)
        inverse = 1.0 / distance
        ux, uy, uz = (o * inverse for o in off)
        angular = (
            None,
            root_three * ux,
            root_three * uy,
            root_three * uz,
            root_fifteen * ux * uy,
            root_fifteen * uy * uz,
            half_root_five * (2.0 * uz * uz - ux * ux - uy * uy),
            root_fifteen * ux * uz,
            half_root_fifteen * (ux * ux - uy * uy),
        )
        angular = [shut if y is None else y * shut for y in angular]
        for k in range(NR):
            radial = jnp.exp(-radial_sharp * jnp.square(distance - k * center_step))
            for m in range(NM):
                kt[p, pl.ds((m * NR + k) * rows, rows), pl.ds(BLK * half, BLK)] = (
                    radial * angular[m]
                ).astype(jnp.bfloat16)

    def two_pairs(step):
        def one(p, _):
            for half in range(2):
                geometry(p, half)
            return 0

        lax.fori_loop(2 * step, 2 * step + 2, one, 0)

    for step, d in enumerate(near_first):
        two_pairs(step)
        feat_copy(d).wait_recv()
        for side in range(2):
            halo_copy(side, d).start()

    for b in range(OWN):
        sendt[b] = feat[:, pl.ds(BLK * place_of[b], BLK)].T
    shift = lax.rem(BLK - z * rows, BLK)
    fown[...] = jnp.concatenate(
        [
            pltpu.roll(feat[:, pl.ds(BLK * place_of[b], BLK)].astype(jnp.float32), shift, 1)[:, :rows]
            for b in range(OWN)
        ]
        + [jnp.zeros((BLK, BLK - OWN * rows), jnp.float32)],
        axis=1,
    )
    own_present = jnp.concatenate(
        [pltpu.roll(boxes[b], shift, 1)[3:4, :rows] for b in range(OWN)]
        + [jnp.zeros((1, BLK - OWN * rows), jnp.float32)],
        axis=1,
    )
    mix_copy.wait()
    for n in range(4):
        mixt[:, pl.ds(BLK * n, BLK)] = mixv[n].T
    for d in range(1, nc):
        w_copy(d).wait_recv()
    for k in range(NR):
        whole = jnp.concatenate([wst[s, :, cz * k : cz * (k + 1)] for s in range(nc)], axis=1)
        for l in range(3):
            wb[l, k] = jnp.broadcast_to(whole[l : l + 1, :], (8, BLK))
        if k == 0:
            readcol[...] = jnp.broadcast_to(whole[3:4, :], (BLK, BLK)).T
    for d in range(nc):
        for side in range(2):
            halo_copy(side, d).wait_recv()
    for side in range(2):
        bit = meta_in[side, 0][5 - side : 6 - side, :] > 0.5
        early = halo[side, :, 0:BLK].astype(jnp.float32)
        late = halo[side, :, BLK : 2 * BLK].astype(jnp.float32)
        sendt[OWN + 2 * side] = jnp.where(bit, late, early).astype(jnp.bfloat16).T
        sendt[OWN + 2 * side + 1] = jnp.where(bit, early, late).astype(jnp.bfloat16).T

    run[PAIRS] = jnp.zeros((NM * rows, BLK), jnp.float32)

    def message(p, _):
        q0 = pairs[0, 1, slot_tile[2 * p]]
        q1 = pairs[0, 1, slot_tile[2 * p + 1]]
        both = jnp.concatenate([sendt[q0], sendt[q1]], axis=0)
        before = lax.rem(p + PAIRS, PAIRS + 1)
        kept = keep[p].astype(jnp.float32)
        part = jnp.dot(kt[p], both, preferred_element_type=jnp.float32)
        for m in range(NM):
            acc = run[before, pl.ds(m * rows, rows), :] * kept
            for k in range(NR):
                w = wb[degree[m], k]
                at = (m * NR + k) * rows
                acc = acc + jnp.concatenate([w] * (rows // 8), axis=0) * part[at : at + rows, :]
            run[p, pl.ds(m * rows, rows), :] = acc
        return 0

    lax.fori_loop(0, PAIRS, message, 0)

    basis = []
    for b in range(OWN):
        slot = last_slot[b]
        den = [run[slot, pl.ds(m * rows, rows), :] for m in range(NM)]
        vec = den[1] * den[1] + den[2] * den[2] + den[3] * den[3]
        ten = sum(den[m] * den[m] for m in range(5, NM)) + den[4] * den[4]
        basis.append(jnp.concatenate([den[0], den[0] * den[0], vec, ten], axis=1))
    basis = jnp.concatenate(
        basis + [jnp.zeros((BLK - OWN * rows, 4 * BLK), jnp.float32)], axis=0
    ).astype(jnp.bfloat16)
    mixed = lax.dot_general(
        mixt[...], basis, (((1,), (1,)), ((), ())), preferred_element_type=jnp.float32
    )
    hidden = fown[...] + mixed / (1.0 + jnp.exp(-mixed))
    energy = jnp.sum(readcol[...] * hidden, axis=0, keepdims=True)
    square = jnp.sum(energy * energy * own_present, axis=1, keepdims=True)
    est[z] = jnp.concatenate(
        [energy, jnp.broadcast_to(square, (1, BLK)), jnp.zeros((6, BLK), jnp.float32)], axis=0
    )

    def e_copy(d):
        return pltpu.make_async_remote_copy(
            src_ref=est.at[z],
            dst_ref=est.at[z],
            send_sem=e_send.at[d],
            recv_sem=e_recv.at[d],
            device_id=chan_peer(d),
            device_id_type=MESH,
        )

    def u_copy(d):
        part = pl.ds(pl.multiple_of(lax.rem(z + d, nc) * cz, cz), cz)
        return pltpu.make_async_remote_copy(
            src_ref=ust_send.at[part],
            dst_ref=ust.at[z],
            send_sem=u_send.at[d],
            recv_sem=u_recv.at[d],
            device_id=chan_peer(d),
            device_id_type=MESH,
        )

    for d in far_first:
        e_copy(d).start()
    ust_send[...] = (hidden * own_present).astype(jnp.bfloat16)
    ust[z] = ust_send[own_rows, :]
    for d in range(1, nc):
        e_copy(d).wait_recv()
    group = est[0, 1:2, :]
    for s in range(1, nc):
        group = group + est[s, 1:2, :]
    atoms = zero_row
    for b in range(OWN):
        atoms = atoms + counts[b].astype(jnp.float32)
    fill6 = jnp.zeros((6, BLK), jnp.float32)
    yst[yi] = jnp.concatenate([group, atoms, fill6], axis=0)

    def y_copy(d):
        return pltpu.make_async_remote_copy(
            src_ref=yst.at[yi],
            dst_ref=yst.at[yi],
            send_sem=y_send.at[d],
            recv_sem=y_recv.at[d],
            device_id=y_peer(d),
            device_id_type=MESH,
        )

    def x_copy(d):
        return pltpu.make_async_remote_copy(
            src_ref=xst.at[xc],
            dst_ref=xst.at[xc],
            send_sem=x_send.at[d],
            recv_sem=x_recv.at[d],
            device_id=x_peer(d),
            device_id_type=MESH,
        )

    for d in range(1, ny):
        y_copy(d).start()
    for d in far_first:
        u_copy(d).start()
    energies = []
    for b in range(OWN):
        line = jnp.concatenate(
            [est[s, 0:1, rows * b : rows * (b + 1)] for s in range(nc)], axis=1
        )
        energies.append(line * boxes[b][3:4, :])
    energies = jnp.concatenate(energies, axis=0)
    for d in range(1, ny):
        y_copy(d).wait_recv()
    plane = yst[0]
    for s in range(1, ny):
        plane = plane + yst[s]
    xst[xc] = plane
    for d in range(1, nxc):
        x_copy(d).start()
    for d in range(1, nc):
        u_copy(d).wait_recv()
    for b in range(OWN):
        upd_out[:, pl.ds(BLK * b, BLK)] = jnp.concatenate(
            [ust[s].astype(jnp.float32)[:, rows * b : rows * (b + 1)] for s in range(nc)], axis=1
        ).astype(jnp.bfloat16)
    for d in range(1, nxc):
        x_copy(d).wait_recv()
    whole = xst[0]
    for s in range(1, nxc):
        whole = whole + xst[s]
    scale = jnp.sqrt(1.0 + whole[0:1, :] / whole[1:2, :])
    energy_out[...] = energies / scale
    scale_out[...] = scale

    for side in range(2):
        meta_copy(side).wait_send()
        for d in range(nc):
            halo_copy(side, d).wait_send()
    for d in range(1, nc):
        feat_copy(d).wait_send()
        w_copy(d).wait_send()
        e_copy(d).wait_send()
        u_copy(d).wait_send()
    for d in range(1, ny):
        y_copy(d).wait_send()
    for d in range(1, nxc):
        x_copy(d).wait_send()


def per_device(
    na, nc, features, positions, block_counts, radial_w, mix_w, read_w, ghost_lists, tile_pairs, tile_count
):
    cz, width = features.shape
    rows = BLK // nc
    ny = max(1, min(8, na // 2))
    nxc = na // ny
    tiles = tile_pairs.shape[1]
    radial_w = radial_w.transpose(1, 0, 2)
    tile_pairs = tile_pairs.transpose(0, 2, 1)
    f32, bf16, i32 = jnp.float32, jnp.bfloat16, jnp.int32
    vm, sm, dma = pltpu.VMEM, pltpu.SMEM, pltpu.SemaphoreType.DMA
    hbm = pl.BlockSpec(memory_space=pltpu.HBM)
    vmem = pl.BlockSpec(memory_space=pltpu.VMEM)
    updated, energies, scale = pl.pallas_call(
        functools.partial(kernel, na, nc),
        out_shape=(
            jax.ShapeDtypeStruct((cz, width), bf16),
            jax.ShapeDtypeStruct((OWN, BLK), f32),
            jax.ShapeDtypeStruct((1, BLK), f32),
        ),
        in_specs=[hbm] * 9,
        out_specs=(vmem, vmem, vmem),
        scratch_shapes=[
            vm((BLK, width), bf16),
            vm((2, BLK, 2 * BLK), bf16),
            vm((3, width), f32),
            vm((4, BLK, BLK), bf16),
            vm((BLK, 4 * BLK), bf16),
            vm((3, NR, cz), f32),
            vm((cz,), f32),
            vm((nc, 8, BLK), f32),
            vm((3, NR, 8, BLK), f32),
            vm((BLK, BLK), f32),
            vm((2, 2, 8, BLK), f32),
            vm((2, 2, 8, BLK), f32),
            vm((2 * OWN, 8, BLK), f32),
            vm((BLK, BLK), f32),
            vm((OWN, 3, rows, BLK), f32),
            vm((2 * OWN, BLK, BLK), bf16),
            vm((PAIRS, NM * NR * rows, 2 * BLK), bf16),
            vm((PAIRS + 1, NM * rows, BLK), f32),
            vm((BLK, BLK), f32),
            vm((BLK, BLK), bf16),
            vm((nc, cz, BLK), bf16),
            vm((nc, 8, BLK), f32),
            vm((ny, 8, BLK), f32),
            vm((nxc, 8, BLK), f32),
            sm((OWN,), i32),
            sm((1, 2, 2), i32),
            sm((1, 2, tiles), i32),
            sm((1,), i32),
            sm((tiles,), i32),
            sm((2 * PAIRS,), i32),
            sm((2 * PAIRS,), i32),
            sm((PAIRS,), i32),
            sm((OWN,), i32),
            dma((12,)),
            dma((nc,)),
            dma((nc,)),
            dma((nc,)),
            dma((nc,)),
            dma((4,)),
            dma((2, nc)),
            dma((2, nc)),
            dma((nc,)),
            dma((nc,)),
            dma((nc,)),
            dma((nc,)),
            dma((max(ny, 2),)),
            dma((max(ny, 2),)),
            dma((max(nxc, 2),)),
            dma((max(nxc, 2),)),
        ],
        compiler_params=pltpu.CompilerParams(
            collective_id=0, has_side_effects=True, vmem_limit_bytes=67043328
        ),
        name="message_layer",
    )(features, positions, block_counts, radial_w, mix_w, read_w, ghost_lists, tile_pairs, tile_count)
    return updated, energies.reshape(width), scale[0, 0]


def solution(mesh):
    in_specs = (
        P("chan", "atoms"),
        P(None, "atoms"),
        P("atoms"),
        P(None, None, "chan"),
        P(),
        P("chan"),
        P("atoms", None, None),
        P("atoms", None, None),
        P("atoms"),
    )
    out_specs = (P("chan", "atoms"), P("atoms"), P())
    step = functools.partial(per_device, mesh.shape["atoms"], mesh.shape["chan"])
    return jax.shard_map(step, mesh=mesh, in_specs=in_specs, out_specs=out_specs, check_vma=False)
```

time: 205 us -> 48.9 us (0.24)
  matrix products: 61.3 us -> 0 us
  Pallas kernels: 0 us -> 44.2 us
  other arithmetic: 36.7 us -> 0 us
  local copies, waits for them, and re-layouts: 38 us -> 1.94 us
  starting transfers between devices: 31.9 us -> 0 us
  blocking collectives: 16.2 us -> 0 us
  waiting for transfers between devices: 15.3 us -> 0 us
    dot_general x14 -> x0, matrix products: 61.3 us -> none  [the longest x6 33.8 us: tile_term(): jnp.einsum('cj,kmij->ckmi', sender_rows, kernel, preferred_element_type=j...]
    pallas_call x0 -> x1, Pallas kernels: none -> 44.2 us  [per_device(): pl.pallas_call(functools.partial(kernel, na, nc), out_shape=(jax.ShapeDty...]
    gather x37 -> x0, local copies, waits for them, and re-layouts: 35.4 us -> none  [the longest x6 7.96 us: one_turn(): receivers = tile_list[tile_ids, 0]]
    all_to_all x2 -> x0, starting transfers between devices: 17.6 us -> none  [copy_for_each(): return lax.all_to_all(copies, axis, split_axis=0, concat_axis=0, tiled=True)]
    all_to_all x1 -> x0, blocking collectives: 16.2 us -> none  [sent_and_summed(): tiles = lax.all_to_all(split_up(x, dim, count), axis, 0, 0, tiled=True)]
    all_to_all x2 -> x0, waiting for transfers between devices: 14.6 us -> none  [copy_for_each(): return lax.all_to_all(copies, axis, split_axis=0, concat_axis=0, tiled=True)]
    ppermute x4 -> x0, starting transfers between devices: 14.3 us -> none  [the longest x2 7.86 us: extended(): lax.ppermute(lax.slice_in_dim(block, 0, width, axis=dim), axis, backward)]
    exp x6 -> x0, other arithmetic: 10.4 us -> none  [tile_kernel(): jnp.exp(-radial_sharp * jnp.square(distance[None] - centers[:, None, None]))]
  transfers between devices with their start and end apart: 6 -> 0, of which waited for: 3 -> 0; matrix products, arithmetic and copies ran while one was open for 3% -> 0% of each run, Pallas kernels for 0% -> 0%
where the time goes in v1:
time: 48.9 us; the launch traced here: 48.6 us
  Pallas kernels  44.2 us (90%)
  between operations  2.46 us (5%)
  local copies, waits for them, and re-layouts  1.94 us (4%)
    pallas_call x1, Pallas kernels, per_device(): pl.pallas_call(functools.partial(kernel, na, nc), out_shape=(jax.ShapeDty...  44.2 us
    unnamed x6, local copies, waits for them, and re-layouts  1.94 us

profile of v1, /device:TPU:1, one launch (start us, length us, event | category | flops | bytes accessed | tf_op | source)
XLA Modules:
  0.0 48.6 jit_solution(9893046019220989225)
XLA Ops:
  1.3 44.2 %message_layer.1 = (bf16[16,512]{1,0:T(8,128)(2,1)}, f32[4,128]{1,0:T(4,128)}, f32[1,128]{1,0:T(1,128)}) custom-call(bf16[16,512]{1,0:T(8,128)(2,1)} %feat_hbm.1, f32[3,512]{1,0:T(4,128)} %pos_hbm.1, s32[4]{0:T(128)} %counts_hbm.1, f32[3,8,16]{2,1,0:T(8,128)} %bitcast.5, bf16[4,128,128]{2,1,0:T(8,128)(2,1)} %mix_hbm.1, f32[16]{0:T(128)} %read_hbm.1, ...), custom_call_target="tpu_custom_call" | custom-call | tf_op jit(solution)/shard_map/message_layer/pallas_call | solution.py:568
  45.5 0.0 copy-start
  45.5 1.3 %copy.16 = bf16[16,512]{1,0:T(8,128)(2,1)} copy(bf16[16,512]{1,0:T(8,128)(2,1)} %get-tuple-element.12) | data formatting | bytes 32768
  46.9 0.0 copy-done
  46.9 0.0 copy-start.1
  46.9 0.6 %copy.17 = f32[512]{0:T(512)} copy(f32[512]{0:T(512)S(1)} %bitcast.6) | data formatting | bytes 4096
  47.4 0.0 copy-done.1
Async XLA Ops:
  45.5 1.3 %copy-start = (f32[4,128]{1,0:T(4,128)S(1)}, f32[4,128]{1,0:T(4,128)}, u32[]{:S(2)}) copy-start(f32[4,128]{1,0:T(4,128)} %get-tuple-element.7) | copy-start | bytes 6148
  46.9 0.6 %copy-start.1 = (f32[1,128]{1,0:T(1,128)S(1)}, f32[1,128]{1,0:T(1,128)}, u32[]{:S(2)}) copy-start(f32[1,128]{1,0:T(1,128)} %get-tuple-element.8) | copy-start | bytes 1540

commit v2 on v1

--- a/solution.py
+++ b/solution.py
@@ -64,8 +64,7 @@
     ust_send,
     ust,
     est,
-    yst,
-    xst,
+    plane,
     counts,
     ghost,
     pairs,
@@ -87,10 +86,8 @@
     u_recv,
     e_send,
     e_recv,
-    y_send,
-    y_recv,
-    x_send,
-    x_recv,
+    plane_sem,
+    ready,
 ):
     cz = feat_hbm.shape[0]
     tiles = pairs.shape[2]
@@ -118,33 +115,6 @@
         return ((other // 2) * (2 * ny) + yi * 2 + lax.rem(other, 2), z)
 
     own_rows = pl.ds(pl.multiple_of(z * cz, cz), cz)
-
-    local = [
-        pltpu.make_async_copy(
-            feat_hbm.at[:, pl.ds(BLK * b, BLK)],
-            feat.at[own_rows, pl.ds(BLK * n, BLK)],
-            local_sem.at[n],
-        )
-        for n, b in enumerate(order)
-    ]
-    pos_copy = pltpu.make_async_copy(pos_hbm, pos, local_sem.at[4])
-    rw_copy = pltpu.make_async_copy(radial_hbm, rw, local_sem.at[5])
-    rd_copy = pltpu.make_async_copy(read_hbm, rd, local_sem.at[6])
-    mix_copy = pltpu.make_async_copy(mix_hbm, mixv, local_sem.at[7])
-    ints = [
-        pltpu.make_async_copy(src, dst, local_sem.at[8 + n])
-        for n, (src, dst) in enumerate(
-            ((counts_hbm, counts), (ghost_hbm, ghost), (pairs_hbm, pairs), (live_hbm, live_count))
-        )
-    ]
-    pos_copy.start()
-    for c in ints:
-        c.start()
-    for c in local:
-        c.start()
-    rw_copy.start()
-    rd_copy.start()
-    mix_copy.start()
 
     barrier = pltpu.get_barrier_semaphore()
     greeted = 0
@@ -161,6 +131,33 @@
         pl.semaphore_signal(barrier, inc=1, device_id=x_peer(d), device_id_type=MESH)
         greeted += 1
 
+    local = [
+        pltpu.make_async_copy(
+            feat_hbm.at[:, pl.ds(BLK * b, BLK)],
+            feat.at[own_rows, pl.ds(BLK * n, BLK)],
+            local_sem.at[n],
+        )
+        for n, b in enumerate(order)
+    ]
+    pos_copy = pltpu.make_async_copy(pos_hbm, pos, local_sem.at[4])
+    rw_copy = pltpu.make_async_copy(radial_hbm, rw, local_sem.at[5])
+    rd_copy = pltpu.make_async_copy(read_hbm, rd, local_sem.at[6])
+    mix_copy = pltpu.make_async_copy(mix_hbm, mixv, local_sem.at[7])
+    ints = [
+        pltpu.make_async_copy(src, dst, local_sem.at[8 + n])
+        for n, (src, dst) in enumerate(
+            ((counts_hbm, counts), (ghost_hbm, ghost), (pairs_hbm, pairs), (live_hbm, live_count))
+        )
+    ]
+    for c in local:
+        c.start()
+    pos_copy.start()
+    for c in ints:
+        c.start()
+    rw_copy.start()
+    rd_copy.start()
+    mix_copy.start()
+
     lane = lax.broadcasted_iota(jnp.int32, (1, BLK), 1)
     for c in ints:
         c.wait()
@@ -194,65 +191,45 @@
 
     total = live_count[0]
 
-    def count(t, acc):
+    sizes = [jnp.int32(0)] * OWN
+    ranks = []
+    for t in range(tiles):
         r = pairs[0, 0, t]
-        alive = t < total
-        rank = jnp.int32(0)
-        out = []
-        for b in range(OWN):
-            hit = jnp.logical_and(alive, r == b)
-            rank = jnp.where(hit, acc[b], rank)
-            out.append(acc[b] + hit.astype(jnp.int32))
-        tile_place[t] = rank
-        return tuple(out)
-
-    sizes = lax.fori_loop(0, tiles, count, (jnp.int32(0),) * OWN)
+        alive = (t < total).astype(jnp.int32)
+        rank = sizes[0]
+        for b in range(1, OWN):
+            rank = jnp.where(r == b, sizes[b], rank)
+        ranks.append(rank)
+        sizes = [n + jnp.where(r == b, alive, 0) for b, n in enumerate(sizes)]
     starts = [jnp.int32(0)]
     for b in range(OWN):
         used = (sizes[b] + 1) >> 1
         last_slot[b] = jnp.maximum(starts[b] + used - 1, 0)
         starts.append(starts[b] + used)
-
-    def settle(t, _):
+    for t in range(tiles):
         r = pairs[0, 0, t]
-        first = jnp.int32(0)
-        for b in range(OWN):
+        first = starts[0]
+        for b in range(1, OWN):
             first = jnp.where(r == b, starts[b], first)
-        spot = 2 * first + tile_place[t]
-        tile_place[t] = jnp.where(t < total, spot, -1)
-        return 0
-
-    lax.fori_loop(0, tiles, settle, 0)
-
-    def fill(s, _):
-        which, alive = jnp.int32(0), jnp.int32(0)
-        for t in range(tiles):
-            hit = (tile_place[t] == s).astype(jnp.int32)
-            which = which + hit * t
-            alive = alive + hit
-        slot_tile[s] = which
-        slot_live[s] = alive
-        return 0
-
-    lax.fori_loop(0, 2 * PAIRS, fill, 0)
-
-    def mark(p, _):
+        tile_place[t] = jnp.where(t < total, 2 * first + ranks[t], -1)
+
+    for p in range(PAIRS):
         same = jnp.int32(1)
         for b in range(OWN):
             same = jnp.where(starts[b] == p, 0, same)
         keep[p] = same
+
+    def fill(n, _):
+        found = [jnp.int32(0)] * 4
+        for t in range(tiles):
+            place = tile_place[t]
+            found = [jnp.where(place == 4 * n + u, t + 32, f) for u, f in enumerate(found)]
+        for u, f in enumerate(found):
+            slot_tile[4 * n + u] = f & 31
+            slot_live[4 * n + u] = f >> 5
         return 0
 
-    lax.fori_loop(0, PAIRS, mark, 0)
-
-    tmat[...] = jnp.zeros((BLK, BLK), jnp.float32)
-    for b in range(OWN):
-        tmat[pl.ds(8 * b, 8), :] = boxes[b]
-    tmat[...] = tmat[...].T
-    mine = tmat[pl.ds(pl.multiple_of(z * rows, rows), rows), :]
-    for b in range(OWN):
-        for d in range(3):
-            rpos[b, d] = jnp.broadcast_to(mine[:, 8 * b + d : 8 * b + d + 1], (rows, BLK))
+    lax.fori_loop(0, PAIRS // 2, fill, 0)
 
     for c in local:
         c.wait()
@@ -301,14 +278,25 @@
 
     far_first = sorted(range(1, nc), key=lambda d: -min(d, nc - d))
     near_first = far_first[::-1]
-    for side in range(2):
-        meta_copy(side).start()
     for d in far_first:
         feat_copy(d).start()
     for side in range(2):
         halo_copy(side, 0).start()
+    for side in range(2):
+        meta_copy(side).start()
     for d in far_first:
         w_copy(d).start()
+    for d in range(1, ny):
+        pl.semaphore_signal(ready, inc=1, device_id=y_peer(d), device_id_type=MESH)
+
+    tmat[...] = jnp.zeros((BLK, BLK), jnp.float32)
+    for b in range(OWN):
+        tmat[pl.ds(8 * b, 8), :] = boxes[b]
+    tmat[...] = tmat[...].T
+    mine = tmat[pl.ds(pl.multiple_of(z * rows, rows), rows), :]
+    for b in range(OWN):
+        for d in range(3):
+            rpos[b, d] = jnp.broadcast_to(mine[:, 8 * b + d : 8 * b + d + 1], (rows, BLK))
 
     for side in range(2):
         meta_copy(side).wait_recv()
@@ -406,25 +394,22 @@
         sendt[OWN + 2 * side] = jnp.where(bit, late, early).astype(jnp.bfloat16).T
         sendt[OWN + 2 * side + 1] = jnp.where(bit, early, late).astype(jnp.bfloat16).T
 
-    run[PAIRS] = jnp.zeros((NM * rows, BLK), jnp.float32)
-
-    def message(p, _):
+    def message(p):
         q0 = pairs[0, 1, slot_tile[2 * p]]
         q1 = pairs[0, 1, slot_tile[2 * p + 1]]
         both = jnp.concatenate([sendt[q0], sendt[q1]], axis=0)
-        before = lax.rem(p + PAIRS, PAIRS + 1)
         kept = keep[p].astype(jnp.float32)
         part = jnp.dot(kt[p], both, preferred_element_type=jnp.float32)
         for m in range(NM):
-            acc = run[before, pl.ds(m * rows, rows), :] * kept
+            acc = 0.0 if p == 0 else run[p - 1, pl.ds(m * rows, rows), :] * kept
             for k in range(NR):
                 w = wb[degree[m], k]
                 at = (m * NR + k) * rows
                 acc = acc + jnp.concatenate([w] * (rows // 8), axis=0) * part[at : at + rows, :]
             run[p, pl.ds(m * rows, rows), :] = acc
-        return 0
-
-    lax.fori_loop(0, PAIRS, message, 0)
+
+    for p in range(PAIRS):
+        message(p)
 
     basis = []
     for b in range(OWN):
@@ -442,9 +427,7 @@
     hidden = fown[...] + mixed / (1.0 + jnp.exp(-mixed))
     energy = jnp.sum(readcol[...] * hidden, axis=0, keepdims=True)
     square = jnp.sum(energy * energy * own_present, axis=1, keepdims=True)
-    est[z] = jnp.concatenate(
-        [energy, jnp.broadcast_to(square, (1, BLK)), jnp.zeros((6, BLK), jnp.float32)], axis=0
-    )
+    est[z] = jnp.where(lane < OWN * rows, energy, jnp.broadcast_to(square, (1, BLK)))
 
     def e_copy(d):
         return pltpu.make_async_remote_copy(
@@ -471,41 +454,36 @@
         e_copy(d).start()
     ust_send[...] = (hidden * own_present).astype(jnp.bfloat16)
     ust[z] = ust_send[own_rows, :]
+    for d in far_first:
+        u_copy(d).start()
     for d in range(1, nc):
         e_copy(d).wait_recv()
-    group = est[0, 1:2, :]
+    group = est[0]
     for s in range(1, nc):
-        group = group + est[s, 1:2, :]
+        group = group + est[s]
     atoms = zero_row
     for b in range(OWN):
         atoms = atoms + counts[b].astype(jnp.float32)
-    fill6 = jnp.zeros((6, BLK), jnp.float32)
-    yst[yi] = jnp.concatenate([group, atoms, fill6], axis=0)
-
-    def y_copy(d):
+    plane[g] = jnp.where(lane < OWN * rows, atoms, group)
+
+    def plane_copy(d):
         return pltpu.make_async_remote_copy(
-            src_ref=yst.at[yi],
-            dst_ref=yst.at[yi],
-            send_sem=y_send.at[d],
-            recv_sem=y_recv.at[d],
-            device_id=y_peer(d),
+            src_ref=plane.at[g],
+            dst_ref=plane.at[g],
+            send_sem=plane_sem.at[0],
+            recv_sem=plane_sem.at[1],
+            device_id=(lax.rem(g + d, na), z),
             device_id_type=MESH,
         )
 
-    def x_copy(d):
-        return pltpu.make_async_remote_copy(
-            src_ref=xst.at[xc],
-            dst_ref=xst.at[xc],
-            send_sem=x_send.at[d],
-            recv_sem=x_recv.at[d],
-            device_id=x_peer(d),
-            device_id_type=MESH,
-        )
-
-    for d in range(1, ny):
-        y_copy(d).start()
-    for d in far_first:
-        u_copy(d).start()
+    if ny > 1:
+        pl.semaphore_wait(ready, ny - 1)
+
+    def tell(n, _):
+        plane_copy(lax.rem(n + (3 * na) // 8, na - 1) + 1).start()
+        return 0
+
+    lax.fori_loop(0, na - 1, tell, 0)
     energies = []
     for b in range(OWN):
         line = jnp.concatenate(
@@ -513,28 +491,25 @@
         )
         energies.append(line * boxes[b][3:4, :])
     energies = jnp.concatenate(energies, axis=0)
-    for d in range(1, ny):
-        y_copy(d).wait_recv()
-    plane = yst[0]
-    for s in range(1, ny):
-        plane = plane + yst[s]
-    xst[xc] = plane
-    for d in range(1, nxc):
-        x_copy(d).start()
     for d in range(1, nc):
         u_copy(d).wait_recv()
     for b in range(OWN):
         upd_out[:, pl.ds(BLK * b, BLK)] = jnp.concatenate(
             [ust[s].astype(jnp.float32)[:, rows * b : rows * (b + 1)] for s in range(nc)], axis=1
         ).astype(jnp.bfloat16)
-    for d in range(1, nxc):
-        x_copy(d).wait_recv()
-    whole = xst[0]
-    for s in range(1, nxc):
-        whole = whole + xst[s]
-    scale = jnp.sqrt(1.0 + whole[0:1, :] / whole[1:2, :])
+    others = pltpu.make_async_remote_copy(
+        src_ref=plane.at[pl.ds(0, na - 1)],
+        dst_ref=plane.at[pl.ds(0, na - 1)],
+        send_sem=plane_sem.at[0],
+        recv_sem=plane_sem.at[1],
+        device_id=(right, z),
+        device_id_type=MESH,
+    )
+    others.wait_recv()
+    whole = jnp.sum(plane[:, 0, :], axis=0, keepdims=True)
+    scale = jnp.sqrt(1.0 + whole[:, BLK - 1 : BLK] / whole[:, 0:1])
     energy_out[...] = energies / scale
-    scale_out[...] = scale
+    scale_out[...] = jnp.broadcast_to(scale, (1, BLK))
 
     for side in range(2):
         meta_copy(side).wait_send()
@@ -545,10 +520,7 @@
         w_copy(d).wait_send()
         e_copy(d).wait_send()
         u_copy(d).wait_send()
-    for d in range(1, ny):
-        y_copy(d).wait_send()
-    for d in range(1, nxc):
-        x_copy(d).wait_send()
+    others.wait_send()
 
 
 def per_device(
@@ -556,8 +528,6 @@
 ):
     cz, width = features.shape
     rows = BLK // nc
-    ny = max(1, min(8, na // 2))
-    nxc = na // ny
     tiles = tile_pairs.shape[1]
     radial_w = radial_w.transpose(1, 0, 2)
     tile_pairs = tile_pairs.transpose(0, 2, 1)
@@ -565,6 +535,10 @@
     vm, sm, dma = pltpu.VMEM, pltpu.SMEM, pltpu.SemaphoreType.DMA
     hbm = pl.BlockSpec(memory_space=pltpu.HBM)
     vmem = pl.BlockSpec(memory_space=pltpu.VMEM)
+    features, positions, block_counts, radial_w, mix_w, read_w, ghost_lists, tile_pairs = (
+        pltpu.with_memory_space_constraint(v, pltpu.HBM)
+        for v in (features, positions, block_counts, radial_w, mix_w, read_w, ghost_lists, tile_pairs)
+    )
     updated, energies, scale = pl.pallas_call(
         functools.partial(kernel, na, nc),
         out_shape=(
@@ -592,13 +566,12 @@
             vm((OWN, 3, rows, BLK), f32),
             vm((2 * OWN, BLK, BLK), bf16),
             vm((PAIRS, NM * NR * rows, 2 * BLK), bf16),
-            vm((PAIRS + 1, NM * rows, BLK), f32),
+            vm((PAIRS, NM * rows, BLK), f32),
             vm((BLK, BLK), f32),
             vm((BLK, BLK), bf16),
             vm((nc, cz, BLK), bf16),
-            vm((nc, 8, BLK), f32),
-            vm((ny, 8, BLK), f32),
-            vm((nxc, 8, BLK), f32),
+            vm((nc, 1, BLK), f32),
+            vm((na, 1, BLK), f32),
             sm((OWN,), i32),
             sm((1, 2, 2), i32),
             sm((1, 2, tiles), i32),
@@ -620,13 +593,11 @@
             dma((nc,)),
             dma((nc,)),
             dma((nc,)),
-            dma((max(ny, 2),)),
-            dma((max(ny, 2),)),
-            dma((max(nxc, 2),)),
-            dma((max(nxc, 2),)),
+            dma((2,)),
+            pltpu.SemaphoreType.REGULAR,
         ],
         compiler_params=pltpu.CompilerParams(
-            collective_id=0, has_side_effects=True, vmem_limit_bytes=67043328
+            collective_id=0, has_side_effects=True, vmem_limit_bytes=48 * 1024 * 1024
         ),
         name="message_layer",
     )(features, positions, block_counts, radial_w, mix_w, read_w, ghost_lists, tile_pairs, tile_count)

time: 48.9 us -> 42.9 us (0.88)
  Pallas kernels: 44.2 us -> 39.1 us
  local copies, waits for them, and re-layouts: 1.94 us -> 1.19 us
    pallas_call x1, Pallas kernels: 44.2 us -> 39.1 us  [per_device(): pl.pallas_call(functools.partial(kernel, na, nc), out_shape=(jax.ShapeDty...]
    unnamed x6 -> x2, local copies, waits for them, and re-layouts: 1.94 us -> 1.19 us
where the time goes in v2:
time: 42.9 us; the launch traced here: 42.8 us
  Pallas kernels  39.1 us (91%)
  between operations  2.45 us (6%)
  local copies, waits for them, and re-layouts  1.19 us (3%)
    pallas_call x1, Pallas kernels, per_device(): pl.pallas_call(functools.partial(kernel, na, nc), out_shape=(jax.ShapeDty...  39.1 us
    unnamed x2, local copies, waits for them, and re-layouts  1.19 us

profile of v2, /device:TPU:1, one launch (start us, length us, event | category | flops | bytes accessed | tf_op | source)
XLA Modules:
  0.0 42.8 jit_solution(1757883443321990248)
XLA Ops:
  1.3 39.1 %message_layer.1 = (bf16[16,512]{1,0:T(8,128)(2,1)S(1)}, f32[4,128]{1,0:T(4,128)S(1)}, f32[1,128]{1,0:T(1,128)S(1)}) custom-call(bf16[16,512]{1,0:T(8,128)(2,1)} %feat_hbm.1, f32[3,512]{1,0:T(4,128)} %pos_hbm.1, s32[4]{0:T(128)} %counts_hbm.1, f32[3,8,16]{2,1,0:T(8,128)} %bitcast.7, bf16[4,128,128]{2,1,0:T(8,128)(2,1)} %mix_hbm.1, f32[16]{0:T(128)} %read_hbm.1, ...), custom_call_target="tpu_custom_call" | custom-call | tf_op jit(solution)/shard_map/message_layer/pallas_call | solution.py:542
  40.4 0.6 %copy.16 = bf16[16,512]{1,0:T(8,128)(2,1)} copy(bf16[16,512]{1,0:T(8,128)(2,1)S(1)} %get-tuple-element.12) | data formatting | bytes 32768
  41.0 0.6 %copy.17 = f32[512]{0:T(512)} copy(f32[512]{0:T(512)S(1)} %bitcast.5) | data formatting | bytes 4096

commit v3 on v2

--- a/solution.py
+++ b/solution.py
@@ -75,17 +75,12 @@
     keep,
     last_slot,
     local_sem,
-    feat_send,
-    feat_recv,
-    w_send,
-    w_recv,
+    feat_sem,
+    w_sem,
     meta_sem,
-    halo_send,
-    halo_recv,
-    u_send,
-    u_recv,
-    e_send,
-    e_recv,
+    halo_sem,
+    u_sem,
+    e_sem,
     plane_sem,
     ready,
 ):
@@ -94,69 +89,105 @@
     rows = BLK // nc
     ny = max(1, min(8, na // 2))
     nx = na // (2 * ny)
-    nxc = 2 * nx
 
     g = lax.axis_index("atoms")
     z = lax.axis_index("chan")
-    left, right = lax.rem(g + na - 1, na), lax.rem(g + 1, na)
-    xi = g // (2 * ny)
-    yi = lax.rem(g // 2, ny)
+
+    def wrap(v, n):
+        return jnp.where(v >= n, v - n, v)
+
+    left, right = wrap(g + na - 1, na), wrap(g + 1, na)
     ci = lax.rem(g, 2)
+    yi = lax.rem(lax.div(g, 2), ny)
+    xi = lax.div(g, 2 * ny)
+
+    def chan_peer(d):
+        return (g, wrap(z + d, nc))
+
+    def y_peer(d):
+        return (xi * (2 * ny) + wrap(yi + d, ny) * 2 + ci, z)
+
     xc = xi * 2 + ci
 
-    def chan_peer(d):
-        return (g, lax.rem(z + d, nc))
-
-    def y_peer(d):
-        return (xi * (2 * ny) + lax.rem(yi + d, ny) * 2 + ci, z)
-
     def x_peer(d):
-        other = lax.rem(xc + d, nxc)
-        return ((other // 2) * (2 * ny) + yi * 2 + lax.rem(other, 2), z)
+        other = wrap(xc + d, 2 * nx)
+        return (lax.div(other, 2) * (2 * ny) + yi * 2 + lax.rem(other, 2), z)
+
+    def hail(sem, device):
+        pl.semaphore_signal(sem, inc=1, device_id=device, device_id_type=MESH)
+
+    def remote(ref, sems, device=None, to=None):
+        return pltpu.make_async_remote_copy(
+            src_ref=ref,
+            dst_ref=ref if to is None else to,
+            send_sem=sems.at[0],
+            recv_sem=sems.at[1],
+            device_id=chan_peer(1) if device is None else device,
+            device_id_type=MESH,
+        )
 
     own_rows = pl.ds(pl.multiple_of(z * cz, cz), cz)
 
-    barrier = pltpu.get_barrier_semaphore()
-    greeted = 0
-    for d in range(1, nc):
-        pl.semaphore_signal(barrier, inc=1, device_id=chan_peer(d), device_id_type=MESH)
-        greeted += 1
-    for other in (left, right):
-        pl.semaphore_signal(barrier, inc=1, device_id=(other, z), device_id_type=MESH)
-        greeted += 1
-    for d in range(1, ny):
-        pl.semaphore_signal(barrier, inc=1, device_id=y_peer(d), device_id_type=MESH)
-        greeted += 1
-    for d in range(1, nxc):
-        pl.semaphore_signal(barrier, inc=1, device_id=x_peer(d), device_id_type=MESH)
-        greeted += 1
-
-    local = [
-        pltpu.make_async_copy(
-            feat_hbm.at[:, pl.ds(BLK * b, BLK)],
-            feat.at[own_rows, pl.ds(BLK * n, BLK)],
-            local_sem.at[n],
-        )
-        for n, b in enumerate(order)
-    ]
-    pos_copy = pltpu.make_async_copy(pos_hbm, pos, local_sem.at[4])
-    rw_copy = pltpu.make_async_copy(radial_hbm, rw, local_sem.at[5])
-    rd_copy = pltpu.make_async_copy(read_hbm, rd, local_sem.at[6])
-    mix_copy = pltpu.make_async_copy(mix_hbm, mixv, local_sem.at[7])
+    pos_copy = pltpu.make_async_copy(pos_hbm, pos, local_sem.at[1])
+    rw_copy = pltpu.make_async_copy(radial_hbm, rw, local_sem.at[2])
+    rd_copy = pltpu.make_async_copy(read_hbm, rd, local_sem.at[3])
+    mix_copy = pltpu.make_async_copy(mix_hbm, mixv, local_sem.at[4])
     ints = [
-        pltpu.make_async_copy(src, dst, local_sem.at[8 + n])
+        pltpu.make_async_copy(src, dst, local_sem.at[5 + n])
         for n, (src, dst) in enumerate(
             ((counts_hbm, counts), (ghost_hbm, ghost), (pairs_hbm, pairs), (live_hbm, live_count))
         )
     ]
-    for c in local:
+
+    for c in ints:
         c.start()
     pos_copy.start()
-    for c in ints:
-        c.start()
+    for n, b in enumerate(order):
+        pltpu.make_async_copy(
+            feat_hbm.at[:, pl.ds(BLK * b, BLK)],
+            feat.at[own_rows, pl.ds(BLK * n, BLK)],
+            local_sem.at[0],
+        ).start()
+    barrier = pltpu.get_barrier_semaphore()
+    far_first = sorted(range(1, nc), key=lambda d: -min(d, nc - d))
+    near = [chan_peer(d) for d in far_first] + [(left, z), (right, z)]
+    near += [y_peer(d) for d in range(1, ny)]
+    near += [x_peer(d) for d in range(1, 2 * nx)]
+    for device in near:
+        hail(barrier, device)
     rw_copy.start()
     rd_copy.start()
     mix_copy.start()
+
+    def feat_copy(d):
+        return pltpu.make_async_remote_copy(
+            src_ref=feat.at[own_rows],
+            dst_ref=feat.at[own_rows],
+            send_sem=feat_sem.at[0],
+            recv_sem=feat_sem.at[min(d, nc - d)],
+            device_id=chan_peer(d),
+            device_id_type=MESH,
+        )
+
+    def feat_wait(level, rows_in):
+        pltpu.make_async_remote_copy(
+            src_ref=feat.at[pl.ds(0, rows_in)],
+            dst_ref=feat.at[pl.ds(0, rows_in)],
+            send_sem=feat_sem.at[0],
+            recv_sem=feat_sem.at[level],
+            device_id=chan_peer(1),
+            device_id_type=MESH,
+        ).wait_recv()
+
+    def pass_on(d):
+        part = pl.ds(pl.multiple_of(wrap(z + d, nc) * cz, cz), cz)
+        for side in range(2):
+            remote(
+                feat.at[part, pl.ds(2 * BLK * side, 2 * BLK)],
+                halo_sem,
+                (left if side == 0 else right, z),
+                halo.at[1 - side, part],
+            ).start()
 
     lane = lax.broadcasted_iota(jnp.int32, (1, BLK), 1)
     for c in ints:
@@ -187,7 +218,7 @@
     read_row = jnp.concatenate(
         [rd[...].reshape(1, cz), jnp.zeros((1, BLK - cz), jnp.float32)], axis=1
     )
-    wst[z] = jnp.concatenate([folded, read_row, jnp.zeros((4, BLK), jnp.float32)], axis=0)
+    wst[z] = jnp.concatenate([folded, read_row], axis=0)
 
     total = live_count[0]
 
@@ -231,63 +262,18 @@
 
     lax.fori_loop(0, PAIRS // 2, fill, 0)
 
-    for c in local:
-        c.wait()
-    pl.semaphore_wait(barrier, greeted)
-
-    def feat_copy(d):
-        return pltpu.make_async_remote_copy(
-            src_ref=feat.at[own_rows],
-            dst_ref=feat.at[own_rows],
-            send_sem=feat_send.at[d],
-            recv_sem=feat_recv.at[d],
-            device_id=chan_peer(d),
-            device_id_type=MESH,
-        )
-
-    def w_copy(d):
-        return pltpu.make_async_remote_copy(
-            src_ref=wst.at[z],
-            dst_ref=wst.at[z],
-            send_sem=w_send.at[d],
-            recv_sem=w_recv.at[d],
-            device_id=chan_peer(d),
-            device_id_type=MESH,
-        )
-
-    def meta_copy(side):
-        return pltpu.make_async_remote_copy(
-            src_ref=meta.at[side],
-            dst_ref=meta_in.at[1 - side],
-            send_sem=meta_sem.at[side],
-            recv_sem=meta_sem.at[3 - side],
-            device_id=(left if side == 0 else right, z),
-            device_id_type=MESH,
-        )
-
-    def halo_copy(side, d):
-        part = pl.ds(pl.multiple_of(lax.rem(z + nc - d, nc) * cz, cz), cz)
-        return pltpu.make_async_remote_copy(
-            src_ref=feat.at[part, pl.ds(2 * BLK * side, 2 * BLK)],
-            dst_ref=halo.at[1 - side, part],
-            send_sem=halo_send.at[side, d],
-            recv_sem=halo_recv.at[1 - side, d],
-            device_id=(left if side == 0 else right, z),
-            device_id_type=MESH,
-        )
-
-    far_first = sorted(range(1, nc), key=lambda d: -min(d, nc - d))
-    near_first = far_first[::-1]
+    pltpu.make_async_copy(feat_hbm, feat.at[own_rows], local_sem.at[0]).wait()
+    pl.semaphore_wait(barrier, len(near))
+    for side in range(2):
+        remote(
+            meta.at[side], meta_sem, (left if side == 0 else right, z), meta_in.at[1 - side]
+        ).start()
     for d in far_first:
         feat_copy(d).start()
-    for side in range(2):
-        halo_copy(side, 0).start()
-    for side in range(2):
-        meta_copy(side).start()
-    for d in far_first:
-        w_copy(d).start()
+        remote(wst.at[z], w_sem, chan_peer(d)).start()
+    pass_on(0)
     for d in range(1, ny):
-        pl.semaphore_signal(ready, inc=1, device_id=y_peer(d), device_id_type=MESH)
+        hail(ready, y_peer(d))
 
     tmat[...] = jnp.zeros((BLK, BLK), jnp.float32)
     for b in range(OWN):
@@ -298,8 +284,7 @@
         for d in range(3):
             rpos[b, d] = jnp.broadcast_to(mine[:, 8 * b + d : 8 * b + d + 1], (rows, BLK))
 
-    for side in range(2):
-        meta_copy(side).wait_recv()
+    remote(meta, meta_sem).wait_recv()
     for side in range(2):
         for n in range(2):
             spos[OWN + 2 * side + n] = meta_in[side, n]
@@ -343,19 +328,19 @@
                     radial * angular[m]
                 ).astype(jnp.bfloat16)
 
-    def two_pairs(step):
-        def one(p, _):
+    def two_pairs(n, _):
+        for u in range(2):
             for half in range(2):
-                geometry(p, half)
-            return 0
-
-        lax.fori_loop(2 * step, 2 * step + 2, one, 0)
-
-    for step, d in enumerate(near_first):
-        two_pairs(step)
-        feat_copy(d).wait_recv()
-        for side in range(2):
-            halo_copy(side, d).start()
+                geometry(2 * n + u, half)
+        return 0
+
+    lax.fori_loop(0, PAIRS // 2, two_pairs, 0)
+    for d in range(1, nc // 2):
+        feat_wait(d, 2 * cz)
+        pass_on(d)
+        pass_on(nc - d)
+    feat_wait(nc // 2, cz)
+    pass_on(nc // 2)
 
     for b in range(OWN):
         sendt[b] = feat[:, pl.ds(BLK * place_of[b], BLK)].T
@@ -376,17 +361,14 @@
     mix_copy.wait()
     for n in range(4):
         mixt[:, pl.ds(BLK * n, BLK)] = mixv[n].T
-    for d in range(1, nc):
-        w_copy(d).wait_recv()
+    remote(wst.at[pl.ds(0, nc - 1)], w_sem).wait_recv()
     for k in range(NR):
         whole = jnp.concatenate([wst[s, :, cz * k : cz * (k + 1)] for s in range(nc)], axis=1)
         for l in range(3):
             wb[l, k] = jnp.broadcast_to(whole[l : l + 1, :], (8, BLK))
         if k == 0:
             readcol[...] = jnp.broadcast_to(whole[3:4, :], (BLK, BLK)).T
-    for d in range(nc):
-        for side in range(2):
-            halo_copy(side, d).wait_recv()
+    remote(halo, halo_sem).wait_recv()
     for side in range(2):
         bit = meta_in[side, 0][5 - side : 6 - side, :] > 0.5
         early = halo[side, :, 0:BLK].astype(jnp.float32)
@@ -429,35 +411,14 @@
     square = jnp.sum(energy * energy * own_present, axis=1, keepdims=True)
     est[z] = jnp.where(lane < OWN * rows, energy, jnp.broadcast_to(square, (1, BLK)))
 
-    def e_copy(d):
-        return pltpu.make_async_remote_copy(
-            src_ref=est.at[z],
-            dst_ref=est.at[z],
-            send_sem=e_send.at[d],
-            recv_sem=e_recv.at[d],
-            device_id=chan_peer(d),
-            device_id_type=MESH,
-        )
-
-    def u_copy(d):
-        part = pl.ds(pl.multiple_of(lax.rem(z + d, nc) * cz, cz), cz)
-        return pltpu.make_async_remote_copy(
-            src_ref=ust_send.at[part],
-            dst_ref=ust.at[z],
-            send_sem=u_send.at[d],
-            recv_sem=u_recv.at[d],
-            device_id=chan_peer(d),
-            device_id_type=MESH,
-        )
-
     for d in far_first:
-        e_copy(d).start()
+        remote(est.at[z], e_sem, chan_peer(d)).start()
     ust_send[...] = (hidden * own_present).astype(jnp.bfloat16)
     ust[z] = ust_send[own_rows, :]
     for d in far_first:
-        u_copy(d).start()
-    for d in range(1, nc):
-        e_copy(d).wait_recv()
+        part = pl.ds(pl.multiple_of(wrap(z + d, nc) * cz, cz), cz)
+        remote(ust_send.at[part], u_sem, chan_peer(d), ust.at[z]).start()
+    remote(est.at[pl.ds(0, nc - 1)], e_sem).wait_recv()
     group = est[0]
     for s in range(1, nc):
         group = group + est[s]
@@ -466,24 +427,11 @@
         atoms = atoms + counts[b].astype(jnp.float32)
     plane[g] = jnp.where(lane < OWN * rows, atoms, group)
 
-    def plane_copy(d):
-        return pltpu.make_async_remote_copy(
-            src_ref=plane.at[g],
-            dst_ref=plane.at[g],
-            send_sem=plane_sem.at[0],
-            recv_sem=plane_sem.at[1],
-            device_id=(lax.rem(g + d, na), z),
-            device_id_type=MESH,
-        )
-
     if ny > 1:
         pl.semaphore_wait(ready, ny - 1)
-
-    def tell(n, _):
-        plane_copy(lax.rem(n + (3 * na) // 8, na - 1) + 1).start()
-        return 0
-
-    lax.fori_loop(0, na - 1, tell, 0)
+    for n in range(na - 1):
+        d = (n + (3 * na) // 8) % (na - 1) + 1
+        remote(plane.at[g], plane_sem, (wrap(g + d, na), z)).start()
     energies = []
     for b in range(OWN):
         line = jnp.concatenate(
@@ -491,35 +439,24 @@
         )
         energies.append(line * boxes[b][3:4, :])
     energies = jnp.concatenate(energies, axis=0)
-    for d in range(1, nc):
-        u_copy(d).wait_recv()
+    remote(ust.at[pl.ds(0, nc - 1)], u_sem).wait_recv()
     for b in range(OWN):
         upd_out[:, pl.ds(BLK * b, BLK)] = jnp.concatenate(
             [ust[s].astype(jnp.float32)[:, rows * b : rows * (b + 1)] for s in range(nc)], axis=1
         ).astype(jnp.bfloat16)
-    others = pltpu.make_async_remote_copy(
-        src_ref=plane.at[pl.ds(0, na - 1)],
-        dst_ref=plane.at[pl.ds(0, na - 1)],
-        send_sem=plane_sem.at[0],
-        recv_sem=plane_sem.at[1],
-        device_id=(right, z),
-        device_id_type=MESH,
-    )
+    others = remote(plane.at[pl.ds(0, na - 1)], plane_sem)
     others.wait_recv()
     whole = jnp.sum(plane[:, 0, :], axis=0, keepdims=True)
     scale = jnp.sqrt(1.0 + whole[:, BLK - 1 : BLK] / whole[:, 0:1])
     energy_out[...] = energies / scale
     scale_out[...] = jnp.broadcast_to(scale, (1, BLK))
 
-    for side in range(2):
-        meta_copy(side).wait_send()
-        for d in range(nc):
-            halo_copy(side, d).wait_send()
-    for d in range(1, nc):
-        feat_copy(d).wait_send()
-        w_copy(d).wait_send()
-        e_copy(d).wait_send()
-        u_copy(d).wait_send()
+    remote(meta, meta_sem).wait_send()
+    remote(halo, halo_sem).wait_send()
+    remote(feat.at[pl.ds(0, (nc - 1) * cz)], feat_sem).wait_send()
+    remote(wst.at[pl.ds(0, nc - 1)], w_sem).wait_send()
+    remote(est.at[pl.ds(0, nc - 1)], e_sem).wait_send()
+    remote(ust.at[pl.ds(0, nc - 1)], u_sem).wait_send()
     others.wait_send()
 
 
@@ -556,7 +493,7 @@
             vm((BLK, 4 * BLK), bf16),
             vm((3, NR, cz), f32),
             vm((cz,), f32),
-            vm((nc, 8, BLK), f32),
+            vm((nc, 4, BLK), f32),
             vm((3, NR, 8, BLK), f32),
             vm((BLK, BLK), f32),
             vm((2, 2, 8, BLK), f32),
@@ -581,18 +518,13 @@
             sm((2 * PAIRS,), i32),
             sm((PAIRS,), i32),
             sm((OWN,), i32),
-            dma((12,)),
-            dma((nc,)),
-            dma((nc,)),
-            dma((nc,)),
-            dma((nc,)),
-            dma((4,)),
-            dma((2, nc)),
-            dma((2, nc)),
-            dma((nc,)),
-            dma((nc,)),
-            dma((nc,)),
-            dma((nc,)),
+            dma((9,)),
+            dma((5,)),
+            dma((2,)),
+            dma((2,)),
+            dma((2,)),
+            dma((2,)),
+            dma((2,)),
             dma((2,)),
             pltpu.SemaphoreType.REGULAR,
         ],

time: 42.9 us -> 40.8 us (0.951)
  Pallas kernels: 39.1 us -> 37 us
    pallas_call x1, Pallas kernels: 39.1 us -> 37 us  [per_device(): pl.pallas_call(functools.partial(kernel, na, nc), out_shape=(jax.ShapeDty...]
where the time goes in v3:
time: 40.8 us; the launch traced here: 40.7 us
  Pallas kernels  37 us (91%)
  between operations  2.45 us (6%)
  local copies, waits for them, and re-layouts  1.19 us (3%)
    pallas_call x1, Pallas kernels, per_device(): pl.pallas_call(functools.partial(kernel, na, nc), out_shape=(jax.ShapeDty...  37 us
    unnamed x2, local copies, waits for them, and re-layouts  1.19 us

profile of v3, /device:TPU:1, one launch (start us, length us, event | category | flops | bytes accessed | tf_op | source)
XLA Modules:
  0.0 40.7 jit_solution(7729322164809955082)
XLA Ops:
  1.3 37.0 %message_layer.1 = (bf16[16,512]{1,0:T(8,128)(2,1)S(1)}, f32[4,128]{1,0:T(4,128)S(1)}, f32[1,128]{1,0:T(1,128)S(1)}) custom-call(bf16[16,512]{1,0:T(8,128)(2,1)} %feat_hbm.1, f32[3,512]{1,0:T(4,128)} %pos_hbm.1, s32[4]{0:T(128)} %counts_hbm.1, f32[3,8,16]{2,1,0:T(8,128)} %bitcast.7, bf16[4,128,128]{2,1,0:T(8,128)(2,1)} %mix_hbm.1, f32[16]{0:T(128)} %read_hbm.1, ...), custom_call_target="tpu_custom_call" | custom-call | tf_op jit(solution)/shard_map/message_layer/pallas_call | solution.py:479
  38.3 0.6 %copy.16 = bf16[16,512]{1,0:T(8,128)(2,1)} copy(bf16[16,512]{1,0:T(8,128)(2,1)S(1)} %get-tuple-element.12) | data formatting | bytes 32768
  38.9 0.6 %copy.17 = f32[512]{0:T(512)} copy(f32[512]{0:T(512)S(1)} %bitcast.5) | data formatting | bytes 4096

commit v4 on v3

--- a/solution.py
+++ b/solution.py
@@ -458,6 +458,19 @@
     remote(est.at[pl.ds(0, nc - 1)], e_sem).wait_send()
     remote(ust.at[pl.ds(0, nc - 1)], u_sem).wait_send()
     others.wait_send()
+
+
+def settle(updated, energies, scale, updated_out, energies_out, scale_out, sems):
+    copies = [
+        pltpu.make_async_copy(src, dst, sems.at[n])
+        for n, (src, dst) in enumerate(
+            ((updated, updated_out), (energies, energies_out), (scale, scale_out))
+        )
+    ]
+    for c in copies:
+        c.start()
+    for c in copies:
+        c.wait()
 
 
 def per_device(
@@ -533,6 +546,19 @@
         ),
         name="message_layer",
     )(features, positions, block_counts, radial_w, mix_w, read_w, ghost_lists, tile_pairs, tile_count)
+    updated, energies, scale = pl.pallas_call(
+        settle,
+        out_shape=(
+            jax.ShapeDtypeStruct((cz, width), bf16),
+            jax.ShapeDtypeStruct((OWN, BLK), f32),
+            jax.ShapeDtypeStruct((1, BLK), f32),
+        ),
+        in_specs=[pl.BlockSpec(memory_space=pl.ANY)] * 3,
+        out_specs=(hbm, hbm, hbm),
+        scratch_shapes=[dma((3,))],
+        compiler_params=pltpu.CompilerParams(vmem_limit_bytes=1024 * 1024),
+        name="settle",
+    )(updated, energies, scale)
     return updated, energies.reshape(width), scale[0, 0]
 
 

time: 40.8 us -> 39.1 us (0.958)
  local copies, waits for them, and re-layouts: 1.19 us -> 0 us
  between operations: 2.45 us -> 1.29 us
  Pallas kernels: 37 us -> 37.7 us
    unnamed x2 -> x0, local copies, waits for them, and re-layouts: 1.19 us -> none
    pallas_call x0 -> x1, Pallas kernels: none -> 0.64 us  [per_device(): pl.pallas_call(settle, out_shape=(jax.ShapeDtypeStruct((cz, width), bf16)...]
where the time goes in v4:
time: 39.1 us; the launch traced here: 39 us
  Pallas kernels  37.7 us (96%)
  between operations  1.29 us (3%)
    pallas_call x1, Pallas kernels, per_device(): pl.pallas_call(functools.partial(kernel, na, nc), out_shape=(jax.ShapeDty...  37 us

profile of v4, /device:TPU:1, one launch (start us, length us, event | category | flops | bytes accessed | tf_op | source)
XLA Modules:
  0.0 39.0 jit_solution(7234335714968894266)
XLA Ops:
  1.3 37.0 %message_layer.1 = (bf16[16,512]{1,0:T(8,128)(2,1)S(1)}, f32[4,128]{1,0:T(4,128)S(1)}, f32[1,128]{1,0:T(1,128)S(1)}) custom-call(bf16[16,512]{1,0:T(8,128)(2,1)} %feat_hbm.1, f32[3,512]{1,0:T(4,128)} %pos_hbm.1, s32[4]{0:T(128)} %counts_hbm.1, f32[3,8,16]{2,1,0:T(8,128)} %bitcast.5, bf16[4,128,128]{2,1,0:T(8,128)(2,1)} %mix_hbm.1, f32[16]{0:T(128)} %read_hbm.1, ...), custom_call_target="tpu_custom_call" | custom-call | tf_op jit(solution)/shard_map/message_layer/pallas_call | solution.py:492
  38.3 0.6 %settle.1 = (bf16[16,512]{1,0:T(8,128)(2,1)}, f32[4,128]{1,0:T(4,128)}, f32[1,128]{1,0:T(1,128)}) custom-call(bf16[16,512]{1,0:T(8,128)(2,1)S(1)} %get-tuple-element.9.updated, f32[4,128]{1,0:T(4,128)S(1)} %get-tuple-element.10.energies, f32[1,128]{1,0:T(1,128)S(1)} %get-tuple-element.11.scale), custom_call_target="tpu_custom_call" | custom-call | tf_op jit(solution)/shard_map/settle/pallas_call | solution.py:549

commit v5 on v4

--- a/solution.py
+++ b/solution.py
@@ -74,7 +74,6 @@
     slot_live,
     keep,
     last_slot,
-    local_sem,
     feat_sem,
     w_sem,
     meta_sem,
@@ -83,6 +82,7 @@
     e_sem,
     plane_sem,
     ready,
+    local_sem,
 ):
     cz = feat_hbm.shape[0]
     tiles = pairs.shape[2]
@@ -120,8 +120,8 @@
         return pltpu.make_async_remote_copy(
             src_ref=ref,
             dst_ref=ref if to is None else to,
-            send_sem=sems.at[0],
-            recv_sem=sems.at[1],
+            send_sem=feat_sem.at[0] if sems.shape[0] == 1 else sems.at[0],
+            recv_sem=sems.at[sems.shape[0] - 1],
             device_id=chan_peer(1) if device is None else device,
             device_id_type=MESH,
         )
@@ -451,13 +451,15 @@
     energy_out[...] = energies / scale
     scale_out[...] = jnp.broadcast_to(scale, (1, BLK))
 
-    remote(meta, meta_sem).wait_send()
-    remote(halo, halo_sem).wait_send()
-    remote(feat.at[pl.ds(0, (nc - 1) * cz)], feat_sem).wait_send()
+    remote(kt.at[0, pl.ds(0, 32 * nc * 2)], halo_sem).wait_send()
     remote(wst.at[pl.ds(0, nc - 1)], w_sem).wait_send()
     remote(est.at[pl.ds(0, nc - 1)], e_sem).wait_send()
     remote(ust.at[pl.ds(0, nc - 1)], u_sem).wait_send()
     others.wait_send()
+
+
+def scoped(na, nc, *refs):
+    pl.run_scoped(lambda sem: kernel(na, nc, *refs, sem), pltpu.SemaphoreType.DMA((9,)))
 
 
 def settle(updated, energies, scale, updated_out, energies_out, scale_out, sems):
@@ -490,7 +492,7 @@
         for v in (features, positions, block_counts, radial_w, mix_w, read_w, ghost_lists, tile_pairs)
     )
     updated, energies, scale = pl.pallas_call(
-        functools.partial(kernel, na, nc),
+        functools.partial(scoped, na, nc),
         out_shape=(
             jax.ShapeDtypeStruct((cz, width), bf16),
             jax.ShapeDtypeStruct((OWN, BLK), f32),
@@ -531,11 +533,10 @@
             sm((2 * PAIRS,), i32),
             sm((PAIRS,), i32),
             sm((OWN,), i32),
-            dma((9,)),
             dma((5,)),
             dma((2,)),
-            dma((2,)),
-            dma((2,)),
+            dma((1,)),
+            dma((1,)),
             dma((2,)),
             dma((2,)),
             dma((2,)),

time: 39.1 us -> 39 us (level)
  no operation moved by 1% of the time
where the time goes in v5:
time: 39 us; the launch traced here: 38.9 us
  Pallas kernels  37.6 us (96%)
  between operations  1.29 us (3%)
    pallas_call x1, Pallas kernels, per_device(): pl.pallas_call(functools.partial(scoped, na, nc), out_shape=(jax.ShapeDty...  36.9 us

profile of v5, /device:TPU:1, one launch (start us, length us, event | category | flops | bytes accessed | tf_op | source)
XLA Modules:
  0.0 38.9 jit_solution(3269608957696449871)
XLA Ops:
  1.3 36.9 %message_layer.1 = (bf16[16,512]{1,0:T(8,128)(2,1)S(1)}, f32[4,128]{1,0:T(4,128)S(1)}, f32[1,128]{1,0:T(1,128)S(1)}) custom-call(bf16[16,512]{1,0:T(8,128)(2,1)} %refs_0_.1, f32[3,512]{1,0:T(4,128)} %refs_1_.1, s32[4]{0:T(128)} %refs_2_.1, f32[3,8,16]{2,1,0:T(8,128)} %bitcast.5, bf16[4,128,128]{2,1,0:T(8,128)(2,1)} %refs_4_.1, f32[16]{0:T(128)} %refs_5_.1, ...), custom_call_target="tpu_custom_call" | custom-call | tf_op jit(solution)/shard_map/message_layer/pallas_call | solution.py:494
  38.2 0.6 %settle.1 = (bf16[16,512]{1,0:T(8,128)(2,1)}, f32[4,128]{1,0:T(4,128)}, f32[1,128]{1,0:T(1,128)}) custom-call(bf16[16,512]{1,0:T(8,128)(2,1)S(1)} %get-tuple-element.9.updated, f32[4,128]{1,0:T(4,128)S(1)} %get-tuple-element.10.energies, f32[1,128]{1,0:T(1,128)S(1)} %get-tuple-element.11.scale), custom_call_target="tpu_custom_call" | custom-call | tf_op jit(solution)/shard_map/settle/pallas_call | solution.py:550

commit v6 on v5

--- a/solution.py
+++ b/solution.py
@@ -462,7 +462,11 @@
     pl.run_scoped(lambda sem: kernel(na, nc, *refs, sem), pltpu.SemaphoreType.DMA((9,)))
 
 
-def settle(updated, energies, scale, updated_out, energies_out, scale_out, sems):
+def settle(*refs):
+    pl.run_scoped(lambda sems: hand_over(*refs, sems), pltpu.SemaphoreType.DMA((3,)))
+
+
+def hand_over(updated, energies, scale, updated_out, energies_out, scale_out, sems):
     copies = [
         pltpu.make_async_copy(src, dst, sems.at[n])
         for n, (src, dst) in enumerate(
@@ -556,7 +560,6 @@
         ),
         in_specs=[pl.BlockSpec(memory_space=pl.ANY)] * 3,
         out_specs=(hbm, hbm, hbm),
-        scratch_shapes=[dma((3,))],
         compiler_params=pltpu.CompilerParams(vmem_limit_bytes=1024 * 1024),
         name="settle",
     )(updated, energies, scale)

time: 39 us -> 39 us (level)
  no operation moved by 1% of the time
where the time goes in v6:
time: 39 us; the launch traced here: 38.8 us
  Pallas kernels  37.5 us (96%)
  between operations  1.29 us (3%)
    pallas_call x1, Pallas kernels, per_device(): pl.pallas_call(functools.partial(scoped, na, nc), out_shape=(jax.ShapeDty...  36.9 us

profile of v6, /device:TPU:1, one launch (start us, length us, event | category | flops | bytes accessed | tf_op | source)
XLA Modules:
  0.0 38.8 jit_solution(13314443267495292287)
XLA Ops:
  1.3 36.9 %message_layer.1 = (bf16[16,512]{1,0:T(8,128)(2,1)S(1)}, f32[4,128]{1,0:T(4,128)S(1)}, f32[1,128]{1,0:T(1,128)S(1)}) custom-call(bf16[16,512]{1,0:T(8,128)(2,1)} %refs_0_.1, f32[3,512]{1,0:T(4,128)} %refs_1_.1, s32[4]{0:T(128)} %refs_2_.1, f32[3,8,16]{2,1,0:T(8,128)} %bitcast.5, bf16[4,128,128]{2,1,0:T(8,128)(2,1)} %refs_4_.1, f32[16]{0:T(128)} %refs_5_.1, ...), custom_call_target="tpu_custom_call" | custom-call | tf_op jit(solution)/shard_map/message_layer/pallas_call | solution.py:498
  38.2 0.6 %settle.1 = (bf16[16,512]{1,0:T(8,128)(2,1)}, f32[4,128]{1,0:T(4,128)}, f32[1,128]{1,0:T(1,128)}) custom-call(bf16[16,512]{1,0:T(8,128)(2,1)S(1)} %get-tuple-element.9.refs_0_, f32[4,128]{1,0:T(4,128)S(1)} %get-tuple-element.10.refs_1_, f32[1,128]{1,0:T(1,128)S(1)} %get-tuple-element.11.refs_2_), custom_call_target="tpu_custom_call" | custom-call | tf_op jit(solution)/shard_map/settle/pallas_call | solution.py:554
